TPU v7x, 128 devices: a whole 4x4x4 slice. The times are simulated.
128 devices in a mesh: pa: 128 (over x, z, y, core).
Axes of the slice: x: 4, y: 4, z: 4, core: 2. Of those that a mesh axis runs over, the one named last changes fastest.
Arguments:
- image_real: float32 [8, 4096, 4096], P(None, 'pa'), may hold values from -6 to 6
- image_imag: float32 [8, 4096, 4096], P(None, 'pa'), may hold values from -6 to 6
Outputs:
- spectrum_real: float32 [8, 4096, 4096], P(None, 'pa')
- spectrum_imag: float32 [8, 4096, 4096], P(None, 'pa')
All inputs are finite; a program needn't handle non-finite values.
Results may differ from a plain program's by a relative error of at most 0.0003.
Values sent between devices are 32-bit elements.
No kernel may reach another device: no remote copies, remote signals or barrier semaphores. Data moves between devices by JAX's collectives and lax.ppermute only.
A program may use at most 256 MiB of HBM per device.

v0:
```python
import functools
import math

import jax
import jax.numpy as jnp
import numpy as np
from jax import lax
from jax.experimental import pallas as pl
from jax.experimental.pallas import tpu as pltpu
from jax.sharding import PartitionSpec as P


N = 4096
FRAMES = 8
SHORT = 32
LONG = 128
LANES = 128
SUB = 8
ROWS = 4 * SHORT * SUB
ROOT_HALF = math.sqrt(0.5)

EDGES = (4, 2, 0, 5, 3, 1)
ORDERS = (
    ((2, 1, 0, 4, 5, 3), (5, 4, 3, 1, 2, 0)),
    ((1, 0, 2, 5, 3, 4), (4, 3, 5, 2, 0, 1)),
    ((0, 2, 1, 3, 4, 5), (3, 5, 4, 0, 1, 2)),
    ((2, 1, 0, 4, 5, 3), (5, 4, 3, 1, 2, 0)),
    ((1, 0, 2, 5, 3, 4), (4, 3, 5, 2, 0, 1)),
    ((0, 2, 1, 3, 4, 5), (3, 5, 4, 0, 1, 2)),
    ((2, 1, 0, 4, 5, 3), (5, 4, 3, 1, 2, 0)),
    ((0, 1, 2, 3, 5, 4), (3, 4, 5, 0, 2, 1)),
)
STEPS = len(EDGES)
SLOTS = 64
GROUPS = ((0, 2), (2, 2), (4, 4))


def recode(chip):
    return chip ^ (chip >> 1 & 21)


def edges_of(frame, core):
    return [EDGES[e] for e in ORDERS[frame][core]]


def edge_pairs(frame, step):
    pairs = []
    for device in range(2 * SLOTS):
        chip, core = divmod(device, 2)
        partner = recode(recode(chip) ^ (1 << edges_of(frame, core)[step]))
        pairs.append((device, partner * 2 + core))
    return pairs


def peer(me, frame, core_bit, steps):
    core = me % 2 ^ core_bit
    masks = [sum(bit << edge for bit, edge in zip(steps, edges_of(frame, c))) for c in range(2)]
    return recode(recode(me // 2) ^ jnp.where(core == 0, *masks)) * 2 + core


def targets(me, frame):
    slot = jnp.arange(2 * SLOTS, dtype=jnp.int32)
    return peer(me, frame, slot >> STEPS, [slot >> (STEPS - 1 - k) & 1 for k in range(STEPS)])


def sources(me, frame):
    slot = jnp.arange(2 * SLOTS, dtype=jnp.int32)
    masks = [sum((slot >> (k + 1) & 1) << edge for k, edge in enumerate(edges_of(frame, c))) for c in range(2)]
    return recode(recode(me // 2) ^ jnp.where(me % 2 == 0, *masks)) * 2 + (me % 2 ^ slot & 1)


def hamming(index):
    return 0.54 - 0.46 * jnp.cos(index.astype(jnp.float32) * (2.0 * math.pi / N))


def column_window():
    window = 0.54 - 0.46 * np.cos(2.0 * np.pi * np.arange(N) / N)
    return window.astype(np.float32)[None]


def twiddles():
    angle = -2.0 * np.pi * (np.arange(SHORT)[:, None] * np.arange(LONG)[None, :]) / N
    wide = np.repeat(np.stack([np.cos(angle), np.sin(angle)]), SUB, axis=1)
    return wide.astype(np.float32)


def long_matrix():
    phase = np.arange(LONG)[:, None] * np.arange(LONG)[None, :] % LONG
    angle = -2.0 * np.pi * phase / LONG
    real, imag = np.cos(angle), np.sin(angle)
    whole = np.block([[real, imag], [-imag, real]]).astype(np.float32)
    high = whole.astype(jnp.bfloat16)
    return np.stack([high, (whole - high.astype(np.float32)).astype(jnp.bfloat16)])


def add(a, b):
    return a[0] + b[0], a[1] + b[1]


def sub(a, b):
    return a[0] - b[0], a[1] - b[1]


def minus_i(a):
    return a[1], -a[0]


def times(a, angle):
    c, s = math.cos(angle), math.sin(angle)
    return a[0] * c - a[1] * s, a[0] * s + a[1] * c


def rotate(a, power):
    power %= 32
    if power == 0:
        return a
    if power == 8:
        return minus_i(a)
    if power == 4:
        return (a[0] + a[1]) * ROOT_HALF, (a[1] - a[0]) * ROOT_HALF
    if power == 12:
        return (a[1] - a[0]) * ROOT_HALF, (a[0] + a[1]) * -ROOT_HALF
    return times(a, -2.0 * math.pi * power / 32)


def dft4(x):
    s, d = add(x[0], x[2]), sub(x[0], x[2])
    t, e = add(x[1], x[3]), sub(x[1], x[3])
    e = minus_i(e)
    return [add(s, t), add(d, e), sub(s, t), sub(d, e)]


def dft8(x):
    even, odd = dft4(x[0::2]), dft4(x[1::2])
    odd = [rotate(v, 4 * k) for k, v in enumerate(odd)]
    return [add(a, b) for a, b in zip(even, odd)] + [sub(a, b) for a, b in zip(even, odd)]


def dft32(load, store):
    parts = []
    for r in range(4):
        part = dft8([load(4 * i + r) for i in range(8)])
        parts.append([rotate(v, r * k) for k, v in enumerate(part)])
    for k in range(8):
        for q, value in enumerate(dft4([parts[r][k] for r in range(4)])):
            store(k + 8 * q, value)


def split(value):
    high = value.astype(jnp.bfloat16)
    return high, (value - high.astype(jnp.float32)).astype(jnp.bfloat16)


def matmul3(high_ref, low_ref, mat_ref, out_ref):
    dot = functools.partial(jnp.dot, preferred_element_type=jnp.float32)
    high, low = high_ref[...], low_ref[...]
    out_ref[...] = dot(high, mat_ref[0]) + dot(low, mat_ref[0]) + dot(high, mat_ref[1])


def tile(i):
    return pl.ds(i * LANES, LANES)


def short_stage(planes, row0, col_ref, tw_ref, z_ref, z_row):
    def load(a):
        w = col_ref[:, tile(a)]
        return tuple(p[pl.ds(row0, SUB), tile(a)] * w for p in planes)

    def store(k, value):
        real, imag = value
        if k:
            c, s = tw_ref[0, pl.ds(k * SUB, SUB), :], tw_ref[1, pl.ds(k * SUB, SUB), :]
            real, imag = real * c - imag * s, real * s + imag * c
        z_ref[0, pl.ds(z_row + k * SUB, SUB), :] = real
        z_ref[1, pl.ds(z_row + k * SUB, SUB), :] = imag

    dft32(load, store)


def matrix_kernel(target_ref, source_ref, base_ref, forward_ref, backward_ref):
    dot = functools.partial(jnp.dot, preferred_element_type=jnp.float32)
    square = (LONG, LONG)
    for frame in range(len(ORDERS)):
        wanted = jnp.broadcast_to(target_ref[pl.ds(frame, 1), :], square)
        pick = (wanted == lax.broadcasted_iota(jnp.int32, square, 0)).astype(jnp.bfloat16)
        wanted = jnp.broadcast_to(source_ref[:, pl.ds(frame, 1)], square)
        place = (wanted == lax.broadcasted_iota(jnp.int32, square, 1)).astype(jnp.bfloat16)
        for part in range(2):
            for half in range(2):
                forward_ref[frame, part, :, tile(half)] = dot(base_ref[part, :, tile(half)], pick).astype(jnp.bfloat16)
                backward_ref[frame, part, tile(half), :] = dot(place, base_ref[part, tile(half), :]).astype(jnp.bfloat16)


def last_kernel(real_ref, imag_ref, out_a_ref, out_b_ref, rows_ref, sem):
    copies = [
        pltpu.make_async_copy(ref.at[:, pl.ds(SHORT - SUB, SUB)], rows_ref.at[plane], sem.at[plane])
        for plane, ref in enumerate((real_ref, imag_ref))
    ]
    for copy in copies:
        copy.start()
    for plane, copy in enumerate(copies):
        copy.wait()
        for frame in range(FRAMES):
            out = (out_a_ref, out_b_ref)[frame // 4]
            out[plane, pl.ds(frame % 4 * 2, 2), :] = rows_ref[plane, frame, pl.ds(SUB - 2, 2), :]


def short_kernel(real_ref, imag_ref, col_ref, tw_ref, z_ref):
    z = z_ref.at[pl.program_id(0)]

    @pl.loop(0, 4)
    def _(block):
        row = pl.multiple_of(block * SUB, SUB)
        short_stage((real_ref.at[0], imag_ref.at[0]), row, col_ref, tw_ref, z, pl.multiple_of(row * SHORT, SUB * SHORT))


def edge_kernel(halo_ref, col_ref, tw_ref, out_ref):
    short_stage((halo_ref.at[0], halo_ref.at[1]), 0, col_ref, tw_ref, out_ref, 0)


def pre_kernel(row_ref, z_ref, edge_ref, mat_ref, keep_ref, send_ref, high_ref, low_ref, y_ref, *, first):
    local = pl.program_id(0)
    frame = first + local
    for plane in range(2):

        def rows(js):
            return z_ref[local, plane, pl.ds(js, LANES, stride=SUB), :]

        def rows_before(js):
            edge = edge_ref[plane, pl.ds(frame % 4 * 2 + js - 6, SHORT, stride=SUB), :]
            return jnp.concatenate([edge, z_ref[local, plane, pl.ds(js, 3 * SHORT, stride=SUB), :]], axis=0)

        before = rows_before(7)
        slope = before - rows_before(6)
        for js in range(SUB):
            now = rows(js)
            new_slope = now - before
            value = new_slope - slope
            before, slope = now, new_slope
            for b in range(4):
                part = value[b * SHORT : (b + 1) * SHORT].reshape(SHORT // SUB, SUB, LANES)
                part = part * row_ref[pl.ds((b * SUB + js) * SUB, SUB), :]
                high, low = split(part.reshape(SHORT, LANES))
                high_ref[pl.ds(js * LANES + b * SHORT, SHORT), tile(plane)] = high
                low_ref[pl.ds(js * LANES + b * SHORT, SHORT), tile(plane)] = low

    matmul3(high_ref, low_ref, mat_ref.at[frame], y_ref)

    for plane in range(2):
        outs = [ref.at[local, plane].reshape(SLOTS * SUB, LANES) for ref in (keep_ref, send_ref)]
        for js in range(SUB):
            piece = y_ref[pl.ds(js * LANES, LANES), tile(plane)].T
            for half, flat in enumerate(outs):
                flat[pl.ds(js, SLOTS, stride=SUB), :] = piece[half * SLOTS : (half + 1) * SLOTS]


def gather_kernel(first_ref, second_ref, keep_ref, send_ref, *, step):
    left = SLOTS // 2 >> step

    @pl.loop(0, SLOTS // 2, step=SUB)
    def _(at):
        base = 2 * at - at % left if left >= SUB else 2 * at
        for half, ref in enumerate((first_ref, second_ref)):
            for plane in range(2):
                for slot in range(SUB):
                    source = base + (slot if left >= SUB else 2 * slot - slot % left)
                    for side, out in enumerate((keep_ref, send_ref)):
                        out[plane, half * (SLOTS // 2) + at + slot] = ref[plane, source + side * left]


def copies_out(wide_ref, outs, sem, frame):
    return [pltpu.make_async_copy(wide_ref.at[plane], outs[plane].at[frame], sem.at[plane]) for plane in range(2)]


def post_kernel(keep_ref, got_ref, tw_ref, mat_ref, *refs, frame):
    wide_ref, sem, high_ref, low_ref, y_ref = refs[-5:]
    if frame:
        copies = copies_out(refs[0], refs[-7:-5], sem, frame - 1)
        for copy in copies:
            copy.start()
    for plane in range(2):
        flats = [ref.at[plane].reshape(SLOTS * SUB, LANES) for ref in (keep_ref, got_ref)]
        for js in range(SUB):
            pieces = [flat[pl.ds(js, SLOTS, stride=SUB), :] for flat in flats]
            high, low = split(jnp.concatenate(pieces, axis=0).T)
            high_ref[pl.ds(js * LANES, LANES), tile(plane)] = high
            low_ref[pl.ds(js * LANES, LANES), tile(plane)] = low

    matmul3(high_ref, low_ref, mat_ref.at[frame], y_ref)

    @pl.loop(0, 4)
    def _(block):
        at = pl.multiple_of(block * SUB, SUB)

        def load(j):
            row = pl.ds(((j % SUB) * 4 + j // SUB) * SHORT + at, SUB)
            real, imag = y_ref[row, tile(0)], y_ref[row, tile(1)]
            if j:
                c, s = tw_ref[0, pl.ds(j * SUB, SUB), :], tw_ref[1, pl.ds(j * SUB, SUB), :]
                real, imag = real * c - imag * s, real * s + imag * c
            return real, imag

        def store(k, value):
            for plane in range(2):
                wide_ref[plane, pl.ds(at, SUB), tile(k)] = value[plane]

        dft32(load, store)

    if frame:
        for copy in copies:
            copy.wait()


def flush_kernel(wide_ref, *refs):
    for copy in copies_out(wide_ref, refs[-3:-1], refs[-1], FRAMES - 1):
        copy.start()
    for copy in copies_out(wide_ref, refs[-3:-1], refs[-1], FRAMES - 1):
        copy.wait()


VMEM = pl.BlockSpec(memory_space=pltpu.VMEM)
PARAMS = pltpu.CompilerParams(vmem_limit_bytes=12 * 2**20)


def cost(flops):
    return pl.CostEstimate(flops=flops, bytes_accessed=2**21, transcendentals=0)


def matrices(target, source):
    shape = jax.ShapeDtypeStruct((len(ORDERS), 2, 2 * LONG, 2 * LONG), jnp.bfloat16)
    return pl.pallas_call(
        matrix_kernel,
        in_specs=[VMEM] * 3,
        out_specs=[VMEM] * 2,
        out_shape=[shape] * 2,
        compiler_params=PARAMS,
        cost_estimate=cost(10**6),
        name="matrices",
    )(target, source, jnp.asarray(long_matrix()))


def in_hbm(*arrays):
    return [pltpu.with_memory_space_constraint(x, pltpu.HBM) for x in arrays]


def last_rows(real, imag):
    half = jax.ShapeDtypeStruct((2, SUB, N), jnp.float32)
    return pl.pallas_call(
        last_kernel,
        in_specs=[pl.BlockSpec(memory_space=pl.ANY)] * 2,
        out_specs=[VMEM] * 2,
        out_shape=[half] * 2,
        scratch_shapes=[pltpu.VMEM((2, FRAMES, SUB, N), jnp.float32), pltpu.SemaphoreType.DMA((2,))],
        compiler_params=PARAMS,
        cost_estimate=cost(10**6),
        name="last",
    )(*in_hbm(real, imag))


def short(first, count, real, imag, col, tw):
    frame = pl.BlockSpec((1, SHORT, N), lambda f: (first + f, 0, 0))
    return pl.pallas_call(
        short_kernel,
        grid=(count,),
        in_specs=[frame, frame, VMEM, VMEM],
        out_specs=VMEM,
        out_shape=jax.ShapeDtypeStruct((count, 2, ROWS, LANES), jnp.float32),
        compiler_params=pltpu.CompilerParams(vmem_limit_bytes=12 * 2**20),
        cost_estimate=cost(10**9),
    )(*in_hbm(real, imag), col, tw)


def edges(halo, col, tw):
    return pl.pallas_call(
        edge_kernel,
        in_specs=[VMEM] * 3,
        out_specs=VMEM,
        out_shape=jax.ShapeDtypeStruct((2, SHORT * SUB, LANES), jnp.float32),
        compiler_params=PARAMS,
        cost_estimate=cost(10**6),
        name="edges",
    )(halo, col, tw)


def pre(first, count, row, z, edge, mat):
    f32 = jnp.float32
    half = jax.ShapeDtypeStruct((count, 2, SLOTS, SUB, LANES), f32)
    return pl.pallas_call(
        functools.partial(pre_kernel, first=first),
        grid=(count,),
        in_specs=[VMEM] * 4,
        out_specs=[VMEM, VMEM],
        out_shape=[half, half],
        scratch_shapes=[
            pltpu.VMEM((ROWS, 2 * LANES), jnp.bfloat16),
            pltpu.VMEM((ROWS, 2 * LANES), jnp.bfloat16),
            pltpu.VMEM((ROWS, 2 * LANES), f32),
        ],
        compiler_params=PARAMS,
        cost_estimate=cost(5 * 10**8 * count),
    )(row, z, edge, mat)


WIDE = jax.ShapeDtypeStruct((2, SHORT, N), jnp.float32)
OUT = jax.ShapeDtypeStruct((FRAMES, SHORT, N), jnp.float32)
ANY = pl.BlockSpec(memory_space=pl.ANY)


def post(frame, keep, got, tw, mat, before, outs):
    out_shape, out_specs = ([OUT] * 2, [ANY] * 2) if frame else ([], [])
    results = pl.pallas_call(
        functools.partial(post_kernel, frame=frame),
        in_specs=[VMEM] * (5 if frame else 4) + [ANY] * len(outs),
        out_specs=out_specs + [VMEM],
        out_shape=out_shape + [WIDE],
        input_output_aliases={5 + i: i for i in range(len(outs))},
        scratch_shapes=[
            pltpu.SemaphoreType.DMA((2,)),
            pltpu.VMEM((ROWS, 2 * LANES), jnp.bfloat16),
            pltpu.VMEM((ROWS, 2 * LANES), jnp.bfloat16),
            pltpu.VMEM((ROWS, 2 * LANES), jnp.float32),
        ],
        compiler_params=PARAMS,
        cost_estimate=cost(10**9),
    )(keep, got, tw, mat, *([before] if frame else []), *outs)
    return results[-1], tuple(results[:-1])


def flush(wide, outs):
    return pl.pallas_call(
        flush_kernel,
        in_specs=[VMEM] + [ANY] * 2,
        out_specs=[ANY] * 2,
        out_shape=[OUT] * 2,
        input_output_aliases={1: 0, 2: 1},
        scratch_shapes=[pltpu.SemaphoreType.DMA((2,))],
        compiler_params=PARAMS,
        cost_estimate=cost(10**6),
        name="flush",
    )(wide, *outs)


def gather(step, first, second):
    half = jax.ShapeDtypeStruct((2, SLOTS, SUB, LANES), jnp.float32)
    (one, at_one), (two, at_two) = first, second

    def kernel(one_ref, two_ref, keep_ref, send_ref):
        gather_kernel(one_ref.at[at_one], two_ref.at[at_two], keep_ref, send_ref, step=step)

    return pl.pallas_call(
        kernel,
        in_specs=[VMEM] * 2,
        out_specs=[VMEM] * 2,
        out_shape=[half] * 2,
        compiler_params=pltpu.CompilerParams(vmem_limit_bytes=2**20),
        cost_estimate=cost(10**5),
        name="gather",
    )(one, two)


def permute(value, pairs):
    return lax.ppermute(value, "pa", pairs)


def exchange(frame, halves):
    for step in range(STEPS):
        keep, send = gather(step, *halves)
        got = permute(send, edge_pairs(frame, step))
        halves = (keep[None], 0), (got[None], 0)
    return keep, got


def on_device(real, imag):
    frames, rows, _ = real.shape
    me = lax.axis_index("pa")
    halos = [permute(last, [(d, d + 1) for d in range(2 * SLOTS - 1)]) for last in last_rows(real, imag)]
    row = hamming(me * rows + jnp.arange(rows, dtype=jnp.int32)) * (1.0 / (math.sqrt(6.0) * N))
    row = jnp.broadcast_to(row[:, None, None], (rows, SUB, LANES)).reshape(rows * SUB, LANES)
    col = jnp.asarray(column_window())
    tw = jnp.asarray(twiddles())
    z = []
    for first, count in GROUPS:
        z.append(short(first, count, real, imag, col, tw))
    forward, backward = matrices(
        jnp.stack([targets(me, f) for f in range(frames)]),
        jnp.stack([sources(me, f) for f in range(frames)], axis=1),
    )
    edge = [edges(halo, col, tw) for halo in halos]
    halves = []
    for (first, count), part in zip(GROUPS, z):
        keep, send = pre(first, count, row, part, edge[first // 4], forward)
        got = permute(send, [(i, i ^ 1) for i in range(2 * SLOTS)])
        halves += [((keep, i), (got, i)) for i in range(count)]
    ends = [exchange(frame, halves[frame]) for frame in range(frames)]
    wide, outs = None, ()
    for frame in range(frames):
        wide, outs = post(frame, *ends[frame], tw, backward, wide, outs)
    return tuple(flush(wide, outs))


def solution(mesh):
    placed = (P(None, "pa", None), P(None, "pa", None))
    return jax.shard_map(on_device, mesh=mesh, in_specs=placed, out_specs=placed, check_vma=False)
```

profile of v0, /device:TPU:4, one launch (start us, length us, event | category | flops | bytes accessed | tf_op | source)
XLA Modules:
  0.0 161.0 jit_solution(7782260281634298200)
XLA Ops:
  4.3 3.6 %collective-permute-start = (f32[2,8,4096]{2,1,0:T(8,128)S(1)}, f32[2,8,4096]{2,1,0:T(8,128)S(1)}, u32[]{:S(2)}, u32[]{:S(2)}) collective-permute-start(f32[2,8,4096]{2,1,0:T(8,128)S(1)} %get-tuple-element.129), channel_id=1, source_target_pairs={{0,1},{1,2},{2,3},{3,4},{4,5},{5,6},{6,7},{7,8},{8,9},{9,10},{10,1... | collective-permute-start | bytes 786440 | tf_op jit(solution)/shard_map/ppermute | solution.py:462
  9.7 2.1 %shard_map.72.z_ref = f32[2,2,1024,128]{3,2,1,0:T(8,128)S(1)} custom-call(f32[8,32,4096]{2,1,0:T(8,128)} %real_ref.7, f32[8,32,4096]{2,1,0:T(8,128)} %imag_ref.7, f32[1,4096]{1,0:T(1,128)S(1)} %copy-done.1, f32[2,256,128]{2,1,0:T(8,128)S(1)} %copy-done), custom_call_target="tpu_custom_call" | custom-call | flops 1000000000 | bytes 2097152 | tf_op jit(solution)/shard_map/pallas_call | solution.py:362
  11.9 3.9 %shard_map.68.z_ref = f32[4,2,1024,128]{3,2,1,0:T(8,128)S(1)} custom-call(f32[8,32,4096]{2,1,0:T(8,128)} %real_ref.7, f32[8,32,4096]{2,1,0:T(8,128)} %imag_ref.7, f32[1,4096]{1,0:T(1,128)S(1)} %copy-done.1, f32[2,256,128]{2,1,0:T(8,128)S(1)} %copy-done), custom_call_target="tpu_custom_call" | custom-call | flops 1000000000 | bytes 2097152 | tf_op jit(solution)/shard_map/pallas_call | solution.py:362
  17.3 3.4 %shard_map.69 = (f32[4,2,64,8,128]{4,3,2,1,0:T(8,128)S(1)}, f32[4,2,64,8,128]{4,3,2,1,0:T(8,128)S(1)}) custom-call(f32[256,128]{1,0:T(8,128)S(1)} %broadcast_in_dim.252.row_ref, f32[4,2,1024,128]{3,2,1,0:T(8,128)S(1)} %shard_map.68.z_ref, f32[2,256,128]{2,1,0:T(8,128)S(1)} %edges.2.edge_ref, bf16[8,2,256,256]{3,2,1,0:T(8,128)(2,1)S(1)} %get-tuple-element.130.mat_ref), custom_call_target="tpu_custom_call" | custom-call | flops 2000000000 | bytes 2097152 | tf_op jit(solution)/shard_map/pallas_call | solution.py:388
  23.3 2.1 %shard_map.70.z_ref = f32[2,2,1024,128]{3,2,1,0:T(8,128)S(1)} custom-call(f32[8,32,4096]{2,1,0:T(8,128)} %real_ref.7, f32[8,32,4096]{2,1,0:T(8,128)} %imag_ref.7, f32[1,4096]{1,0:T(1,128)S(1)} %copy-done.1, f32[2,256,128]{2,1,0:T(8,128)S(1)} %copy-done), custom_call_target="tpu_custom_call" | custom-call | flops 1000000000 | bytes 2097152 | tf_op jit(solution)/shard_map/pallas_call | solution.py:362
  31.7 4.9 %collective-permute-done.47 = f32[2,64,8,128]{3,2,1,0:T(8,128)S(1)} collective-permute-done((f32[2,64,8,128]{3,2,1,0:T(8,128)S(1)}, f32[2,64,8,128]{3,2,1,0:T(8,128)S(1)}, u32[]{:S(2)}, u32[]{:S(2)}) %collective-permute-start.47) | collective-permute-done | bytes 524320 | tf_op jit(solution)/shard_map/ppermute | solution.py:462
  52.2 5.0 %collective-permute-done.20 = f32[2,64,8,128]{3,2,1,0:T(8,128)S(1)} collective-permute-done((f32[2,64,8,128]{3,2,1,0:T(8,128)S(1)}, f32[2,64,8,128]{3,2,1,0:T(8,128)S(1)}, u32[]{:S(2)}, u32[]{:S(2)}) %collective-permute-start.20) | collective-permute-done | bytes 524320 | tf_op jit(solution)/shard_map/ppermute | solution.py:462
  62.3 2.5 %collective-permute-start.50 = (f32[2,64,8,128]{3,2,1,0:T(8,128)S(1)}, f32[2,64,8,128]{3,2,1,0:T(8,128)S(1)}, u32[]{:S(2)}, u32[]{:S(2)}) collective-permute-start(f32[2,64,8,128]{3,2,1,0:T(8,128)S(1)} %get-tuple-element.230), channel_id=1, source_target_pairs={{0,24},{1,9},{2,26},{3,11},{4,28},{5,13},{6,30},{7,15},{8,16},{9,1... | collective-permute-start | bytes 1572872 | tf_op jit(solution)/shard_map/ppermute | solution.py:462
  67.0 3.0 %collective-permute-done.8 = f32[2,64,8,128]{3,2,1,0:T(8,128)S(1)} collective-permute-done((f32[2,64,8,128]{3,2,1,0:T(8,128)S(1)}, f32[2,64,8,128]{3,2,1,0:T(8,128)S(1)}, u32[]{:S(2)}, u32[]{:S(2)}) %collective-permute-start.8) | collective-permute-done | bytes 524320 | tf_op jit(solution)/shard_map/ppermute | solution.py:462
  70.0 2.2 %collective-permute-start.31 = (f32[2,64,8,128]{3,2,1,0:T(8,128)S(1)}, f32[2,64,8,128]{3,2,1,0:T(8,128)S(1)}, u32[]{:S(2)}, u32[]{:S(2)}) collective-permute-start(f32[2,64,8,128]{3,2,1,0:T(8,128)S(1)} %get-tuple-element.192), channel_id=1, source_target_pairs={{0,24},{1,9},{2,26},{3,11},{4,28},{5,13},{6,30},{7,15},{8,16},{9,1... | collective-permute-start | bytes 1572872 | tf_op jit(solution)/shard_map/ppermute | solution.py:462
  75.8 3.9 %collective-permute-start.9 = (f32[2,64,8,128]{3,2,1,0:T(8,128)S(1)}, f32[2,64,8,128]{3,2,1,0:T(8,128)S(1)}, u32[]{:S(2)}, u32[]{:S(2)}) collective-permute-start(f32[2,64,8,128]{3,2,1,0:T(8,128)S(1)} %get-tuple-element.149), channel_id=1, source_target_pairs={{0,8},{1,25},{2,10},{3,27},{4,12},{5,29},{6,14},{7,31},{8,0},{9,17... | collective-permute-start | bytes 1572872 | tf_op jit(solution)/shard_map/ppermute | solution.py:462
  84.2 2.6 %collective-permute-done.15 = f32[2,64,8,128]{3,2,1,0:T(8,128)S(1)} collective-permute-done((f32[2,64,8,128]{3,2,1,0:T(8,128)S(1)}, f32[2,64,8,128]{3,2,1,0:T(8,128)S(1)}, u32[]{:S(2)}, u32[]{:S(2)}) %collective-permute-start.15) | collective-permute-done | bytes 524320 | tf_op jit(solution)/shard_map/ppermute | solution.py:462
  86.9 6.4 %collective-permute-start.16 = (f32[2,64,8,128]{3,2,1,0:T(8,128)S(1)}, f32[2,64,8,128]{3,2,1,0:T(8,128)S(1)}, u32[]{:S(2)}, u32[]{:S(2)}) collective-permute-start(f32[2,64,8,128]{3,2,1,0:T(8,128)S(1)} %get-tuple-element.163), channel_id=1, source_target_pairs={{0,8},{1,25},{2,10},{3,27},{4,12},{5,29},{6,14},{7,31},{8,0},{9,17... | collective-permute-start | bytes 1572872 | tf_op jit(solution)/shard_map/ppermute | solution.py:462
  95.1 4.5 %collective-permute-start.4 = (f32[2,64,8,128]{3,2,1,0:T(8,128)S(1)}, f32[2,64,8,128]{3,2,1,0:T(8,128)S(1)}, u32[]{:S(2)}, u32[]{:S(2)}) collective-permute-start(f32[2,64,8,128]{3,2,1,0:T(8,128)S(1)} %get-tuple-element.138), channel_id=1, source_target_pairs={{0,2},{1,7},{2,0},{3,5},{4,6},{5,3},{6,4},{7,1},{8,10},{9,15},{10,... | collective-permute-start | bytes 1572872 | tf_op jit(solution)/shard_map/ppermute | solution.py:462
  99.8 3.8 %collective-permute-start.38 = (f32[2,64,8,128]{3,2,1,0:T(8,128)S(1)}, f32[2,64,8,128]{3,2,1,0:T(8,128)S(1)}, u32[]{:S(2)}, u32[]{:S(2)}) collective-permute-start(f32[2,64,8,128]{3,2,1,0:T(8,128)S(1)} %get-tuple-element.206), channel_id=1, source_target_pairs={{0,24},{1,9},{2,26},{3,11},{4,28},{5,13},{6,30},{7,15},{8,16},{9,1... | collective-permute-start | bytes 1572872 | tf_op jit(solution)/shard_map/ppermute | solution.py:462
  107.4 5.1 %collective-permute-done.4 = f32[2,64,8,128]{3,2,1,0:T(8,128)S(1)} collective-permute-done((f32[2,64,8,128]{3,2,1,0:T(8,128)S(1)}, f32[2,64,8,128]{3,2,1,0:T(8,128)S(1)}, u32[]{:S(2)}, u32[]{:S(2)}) %collective-permute-start.4) | collective-permute-done | bytes 524320 | tf_op jit(solution)/shard_map/ppermute | solution.py:462
  112.5 3.7 %collective-permute-start.11 = (f32[2,64,8,128]{3,2,1,0:T(8,128)S(1)}, f32[2,64,8,128]{3,2,1,0:T(8,128)S(1)}, u32[]{:S(2)}, u32[]{:S(2)}) collective-permute-start(f32[2,64,8,128]{3,2,1,0:T(8,128)S(1)} %get-tuple-element.153), channel_id=1, source_target_pairs={{0,24},{1,9},{2,26},{3,11},{4,28},{5,13},{6,30},{7,15},{8,16},{9,1... | collective-permute-start | bytes 1572872 | tf_op jit(solution)/shard_map/ppermute | solution.py:462
  121.0 2.3 %collective-permute-done.11 = f32[2,64,8,128]{3,2,1,0:T(8,128)S(1)} collective-permute-done((f32[2,64,8,128]{3,2,1,0:T(8,128)S(1)}, f32[2,64,8,128]{3,2,1,0:T(8,128)S(1)}, u32[]{:S(2)}, u32[]{:S(2)}) %collective-permute-start.11) | collective-permute-done | bytes 524320 | tf_op jit(solution)/shard_map/ppermute | solution.py:462
  123.3 3.2 %collective-permute-start.18 = (f32[2,64,8,128]{3,2,1,0:T(8,128)S(1)}, f32[2,64,8,128]{3,2,1,0:T(8,128)S(1)}, u32[]{:S(2)}, u32[]{:S(2)}) collective-permute-start(f32[2,64,8,128]{3,2,1,0:T(8,128)S(1)} %get-tuple-element.167), channel_id=1, source_target_pairs={{0,24},{1,9},{2,26},{3,11},{4,28},{5,13},{6,30},{7,15},{8,16},{9,1... | collective-permute-start | bytes 1572872 | tf_op jit(solution)/shard_map/ppermute | solution.py:462
  128.7 2.4 %collective-permute-done.52.got_ref = f32[2,64,8,128]{3,2,1,0:T(8,128)S(1)} collective-permute-done((f32[2,64,8,128]{3,2,1,0:T(8,128)S(1)}, f32[2,64,8,128]{3,2,1,0:T(8,128)S(1)}, u32[]{:S(2)}, u32[]{:S(2)}) %collective-permute-start.52) | collective-permute-done | bytes 524320 | tf_op jit(solution)/shard_map/ppermute | solution.py:462
  134.6 2.1 %collective-permute-done.24 = f32[2,64,8,128]{3,2,1,0:T(8,128)S(1)} collective-permute-done((f32[2,64,8,128]{3,2,1,0:T(8,128)S(1)}, f32[2,64,8,128]{3,2,1,0:T(8,128)S(1)}, u32[]{:S(2)}, u32[]{:S(2)}) %collective-permute-start.24) | collective-permute-done | bytes 524320 | tf_op jit(solution)/shard_map/ppermute | solution.py:462
  140.2 2.5 %collective-permute-done.6 = f32[2,64,8,128]{3,2,1,0:T(8,128)S(1)} collective-permute-done((f32[2,64,8,128]{3,2,1,0:T(8,128)S(1)}, f32[2,64,8,128]{3,2,1,0:T(8,128)S(1)}, u32[]{:S(2)}, u32[]{:S(2)}) %collective-permute-start.6) | collective-permute-done | bytes 524320 | tf_op jit(solution)/shard_map/ppermute | solution.py:462
  144.0 4.4 %collective-permute-done.39.got_ref = f32[2,64,8,128]{3,2,1,0:T(8,128)S(1)} collective-permute-done((f32[2,64,8,128]{3,2,1,0:T(8,128)S(1)}, f32[2,64,8,128]{3,2,1,0:T(8,128)S(1)}, u32[]{:S(2)}, u32[]{:S(2)}) %collective-permute-start.39) | collective-permute-done | bytes 524320 | tf_op jit(solution)/shard_map/ppermute | solution.py:462
  156.3 2.4 %collective-permute-done.7.got_ref = f32[2,64,8,128]{3,2,1,0:T(8,128)S(1)} collective-permute-done((f32[2,64,8,128]{3,2,1,0:T(8,128)S(1)}, f32[2,64,8,128]{3,2,1,0:T(8,128)S(1)}, u32[]{:S(2)}, u32[]{:S(2)}) %collective-permute-start.7) | collective-permute-done | bytes 524320 | tf_op jit(solution)/shard_map/ppermute | solution.py:462
  (166 shorter events, 77.3 us)
Async XLA Ops:
  2.4 18.4 %collective-permute-start.26 = (f32[2,8,4096]{2,1,0:T(8,128)S(1)}, f32[2,8,4096]{2,1,0:T(8,128)S(1)}, u32[]{:S(2)}, u32[]{:S(2)}) collective-permute-start(f32[2,8,4096]{2,1,0:T(8,128)S(1)} %get-tuple-element.182), channel_id=1, source_target_pairs={{0,1},{1,2},{2,3},{3,4},{4,5},{5,6},{6,7},{7,8},{8,9},{9,10},{10,1... | collective-permute-start | bytes 786440 | tf_op jit(solution)/shard_map/ppermute | solution.py:462
  20.7 22.2 %collective-permute-start.1 = (f32[4,2,64,8,128]{4,3,2,1,0:T(8,128)S(1)}, f32[4,2,64,8,128]{4,3,2,1,0:T(8,128)S(1)}, u32[]{:S(2)}, u32[]{:S(2)}) collective-permute-start(f32[4,2,64,8,128]{4,3,2,1,0:T(8,128)S(1)} %get-tuple-element.132), channel_id=1, source_target_pairs={{0,1},{1,0},{2,3},{3,2},{4,5},{5,4},{6,7},{7,6},{8,9},{9,8},{10,11... | collective-permute-start | bytes 6291464 | tf_op jit(solution)/shard_map/ppermute | solution.py:462
  43.0 14.1 %collective-permute-start.20 = (f32[2,64,8,128]{3,2,1,0:T(8,128)S(1)}, f32[2,64,8,128]{3,2,1,0:T(8,128)S(1)}, u32[]{:S(2)}, u32[]{:S(2)}) collective-permute-start(f32[2,64,8,128]{3,2,1,0:T(8,128)S(1)} %get-tuple-element.171), channel_id=1, source_target_pairs={{0,8},{1,25},{2,10},{3,27},{4,12},{5,29},{6,14},{7,31},{8,0},{9,17... | collective-permute-start | bytes 1572872 | tf_op jit(solution)/shard_map/ppermute | solution.py:462
  48.6 13.7 %collective-permute-start.43 = (f32[2,64,8,128]{3,2,1,0:T(8,128)S(1)}, f32[2,64,8,128]{3,2,1,0:T(8,128)S(1)}, u32[]{:S(2)}, u32[]{:S(2)}) collective-permute-start(f32[2,64,8,128]{3,2,1,0:T(8,128)S(1)} %get-tuple-element.216), channel_id=1, source_target_pairs={{0,2},{1,7},{2,0},{3,5},{4,6},{5,3},{6,4},{7,1},{8,10},{9,15},{10,... | collective-permute-start | bytes 1572872 | tf_op jit(solution)/shard_map/ppermute | solution.py:462
  51.6 13.3 %collective-permute-start.36 = (f32[2,64,8,128]{3,2,1,0:T(8,128)S(1)}, f32[2,64,8,128]{3,2,1,0:T(8,128)S(1)}, u32[]{:S(2)}, u32[]{:S(2)}) collective-permute-start(f32[2,64,8,128]{3,2,1,0:T(8,128)S(1)} %get-tuple-element.202), channel_id=1, source_target_pairs={{0,8},{1,25},{2,10},{3,27},{4,12},{5,29},{6,14},{7,31},{8,0},{9,17... | collective-permute-start | bytes 1572872 | tf_op jit(solution)/shard_map/ppermute | solution.py:462
  60.7 13.6 %collective-permute-start.2 = (f32[2,64,8,128]{3,2,1,0:T(8,128)S(1)}, f32[2,64,8,128]{3,2,1,0:T(8,128)S(1)}, u32[]{:S(2)}, u32[]{:S(2)}) collective-permute-start(f32[2,64,8,128]{3,2,1,0:T(8,128)S(1)} %get-tuple-element.134), channel_id=1, source_target_pairs={{0,32},{1,97},{2,34},{3,99},{4,36},{5,101},{6,38},{7,103},{8,40},{... | collective-permute-start | bytes 1572872 | tf_op jit(solution)/shard_map/ppermute | solution.py:462
  79.8 13.6 %collective-permute-start.3 = (f32[2,64,8,128]{3,2,1,0:T(8,128)S(1)}, f32[2,64,8,128]{3,2,1,0:T(8,128)S(1)}, u32[]{:S(2)}, u32[]{:S(2)}) collective-permute-start(f32[2,64,8,128]{3,2,1,0:T(8,128)S(1)} %get-tuple-element.136), channel_id=1, source_target_pairs={{0,8},{1,25},{2,10},{3,27},{4,12},{5,29},{6,14},{7,31},{8,0},{9,17... | collective-permute-start | bytes 1572872 | tf_op jit(solution)/shard_map/ppermute | solution.py:462
  81.5 13.6 %collective-permute-start.51 = (f32[2,64,8,128]{3,2,1,0:T(8,128)S(1)}, f32[2,64,8,128]{3,2,1,0:T(8,128)S(1)}, u32[]{:S(2)}, u32[]{:S(2)}) collective-permute-start(f32[2,64,8,128]{3,2,1,0:T(8,128)S(1)} %get-tuple-element.232), channel_id=1, source_target_pairs={{0,6},{1,3},{2,4},{3,1},{4,2},{5,7},{6,0},{7,5},{8,14},{9,11},{10,... | collective-permute-start | bytes 1572872 | tf_op jit(solution)/shard_map/ppermute | solution.py:462
  83.5 16.2 %collective-permute-start.45 = (f32[2,64,8,128]{3,2,1,0:T(8,128)S(1)}, f32[2,64,8,128]{3,2,1,0:T(8,128)S(1)}, u32[]{:S(2)}, u32[]{:S(2)}) collective-permute-start(f32[2,64,8,128]{3,2,1,0:T(8,128)S(1)} %get-tuple-element.220), channel_id=1, source_target_pairs={{0,96},{1,33},{2,98},{3,35},{4,100},{5,37},{6,102},{7,39},{8,104},... | collective-permute-start | bytes 1572872 | tf_op jit(solution)/shard_map/ppermute | solution.py:462
  86.8 16.8 %collective-permute-start.22 = (f32[2,64,8,128]{3,2,1,0:T(8,128)S(1)}, f32[2,64,8,128]{3,2,1,0:T(8,128)S(1)}, u32[]{:S(2)}, u32[]{:S(2)}) collective-permute-start(f32[2,64,8,128]{3,2,1,0:T(8,128)S(1)} %get-tuple-element.175), channel_id=1, source_target_pairs={{0,2},{1,7},{2,0},{3,5},{4,6},{5,3},{6,4},{7,1},{8,10},{9,15},{10,... | collective-permute-start | bytes 1572872 | tf_op jit(solution)/shard_map/ppermute | solution.py:462
  86.9 18.8 %collective-permute-start.16 = (f32[2,64,8,128]{3,2,1,0:T(8,128)S(1)}, f32[2,64,8,128]{3,2,1,0:T(8,128)S(1)}, u32[]{:S(2)}, u32[]{:S(2)}) collective-permute-start(f32[2,64,8,128]{3,2,1,0:T(8,128)S(1)} %get-tuple-element.163), channel_id=1, source_target_pairs={{0,8},{1,25},{2,10},{3,27},{4,12},{5,29},{6,14},{7,31},{8,0},{9,17... | collective-permute-start | bytes 1572872 | tf_op jit(solution)/shard_map/ppermute | solution.py:462
  93.4 13.8 %collective-permute-start.10 = (f32[2,64,8,128]{3,2,1,0:T(8,128)S(1)}, f32[2,64,8,128]{3,2,1,0:T(8,128)S(1)}, u32[]{:S(2)}, u32[]{:S(2)}) collective-permute-start(f32[2,64,8,128]{3,2,1,0:T(8,128)S(1)} %get-tuple-element.151), channel_id=1, source_target_pairs={{0,32},{1,97},{2,34},{3,99},{4,36},{5,101},{6,38},{7,103},{8,40},{... | collective-permute-start | bytes 1572872 | tf_op jit(solution)/shard_map/ppermute | solution.py:462
  95.1 17.3 %collective-permute-start.4 = (f32[2,64,8,128]{3,2,1,0:T(8,128)S(1)}, f32[2,64,8,128]{3,2,1,0:T(8,128)S(1)}, u32[]{:S(2)}, u32[]{:S(2)}) collective-permute-start(f32[2,64,8,128]{3,2,1,0:T(8,128)S(1)} %get-tuple-element.138), channel_id=1, source_target_pairs={{0,2},{1,7},{2,0},{3,5},{4,6},{5,3},{6,4},{7,1},{8,10},{9,15},{10,... | collective-permute-start | bytes 1572872 | tf_op jit(solution)/shard_map/ppermute | solution.py:462
  99.8 16.5 %collective-permute-start.38 = (f32[2,64,8,128]{3,2,1,0:T(8,128)S(1)}, f32[2,64,8,128]{3,2,1,0:T(8,128)S(1)}, u32[]{:S(2)}, u32[]{:S(2)}) collective-permute-start(f32[2,64,8,128]{3,2,1,0:T(8,128)S(1)} %get-tuple-element.206), channel_id=1, source_target_pairs={{0,24},{1,9},{2,26},{3,11},{4,28},{5,13},{6,30},{7,15},{8,16},{9,1... | collective-permute-start | bytes 1572872 | tf_op jit(solution)/shard_map/ppermute | solution.py:462
  105.7 14.0 %collective-permute-start.23 = (f32[2,64,8,128]{3,2,1,0:T(8,128)S(1)}, f32[2,64,8,128]{3,2,1,0:T(8,128)S(1)}, u32[]{:S(2)}, u32[]{:S(2)}) collective-permute-start(f32[2,64,8,128]{3,2,1,0:T(8,128)S(1)} %get-tuple-element.177), channel_id=1, source_target_pairs={{0,6},{1,3},{2,4},{3,1},{4,2},{5,7},{6,0},{7,5},{8,14},{9,11},{10,... | collective-permute-start | bytes 1572872 | tf_op jit(solution)/shard_map/ppermute | solution.py:462
  107.2 13.7 %collective-permute-start.17 = (f32[2,64,8,128]{3,2,1,0:T(8,128)S(1)}, f32[2,64,8,128]{3,2,1,0:T(8,128)S(1)}, u32[]{:S(2)}, u32[]{:S(2)}) collective-permute-start(f32[2,64,8,128]{3,2,1,0:T(8,128)S(1)} %get-tuple-element.165), channel_id=1, source_target_pairs={{0,96},{1,33},{2,98},{3,35},{4,100},{5,37},{6,102},{7,39},{8,104},... | collective-permute-start | bytes 1572872 | tf_op jit(solution)/shard_map/ppermute | solution.py:462
  116.4 14.7 %collective-permute-start.52 = (f32[2,64,8,128]{3,2,1,0:T(8,128)S(1)}, f32[2,64,8,128]{3,2,1,0:T(8,128)S(1)}, u32[]{:S(2)}, u32[]{:S(2)}) collective-permute-start(f32[2,64,8,128]{3,2,1,0:T(8,128)S(1)} %get-tuple-element.234), channel_id=1, source_target_pairs={{0,96},{1,33},{2,98},{3,35},{4,100},{5,37},{6,102},{7,39},{8,104},... | collective-permute-start | bytes 1572872 | tf_op jit(solution)/shard_map/ppermute | solution.py:462
  119.7 13.4 %collective-permute-start.46 = (f32[2,64,8,128]{3,2,1,0:T(8,128)S(1)}, f32[2,64,8,128]{3,2,1,0:T(8,128)S(1)}, u32[]{:S(2)}, u32[]{:S(2)}) collective-permute-start(f32[2,64,8,128]{3,2,1,0:T(8,128)S(1)} %get-tuple-element.222), channel_id=1, source_target_pairs={{0,24},{1,9},{2,26},{3,11},{4,28},{5,13},{6,30},{7,15},{8,16},{9,1... | collective-permute-start | bytes 1572872 | tf_op jit(solution)/shard_map/ppermute | solution.py:462
  120.9 15.9 %collective-permute-start.24 = (f32[2,64,8,128]{3,2,1,0:T(8,128)S(1)}, f32[2,64,8,128]{3,2,1,0:T(8,128)S(1)}, u32[]{:S(2)}, u32[]{:S(2)}) collective-permute-start(f32[2,64,8,128]{3,2,1,0:T(8,128)S(1)} %get-tuple-element.179), channel_id=1, source_target_pairs={{0,96},{1,33},{2,98},{3,35},{4,100},{5,37},{6,102},{7,39},{8,104},... | collective-permute-start | bytes 1572872 | tf_op jit(solution)/shard_map/ppermute | solution.py:462
  123.3 13.5 %collective-permute-start.18 = (f32[2,64,8,128]{3,2,1,0:T(8,128)S(1)}, f32[2,64,8,128]{3,2,1,0:T(8,128)S(1)}, u32[]{:S(2)}, u32[]{:S(2)}) collective-permute-start(f32[2,64,8,128]{3,2,1,0:T(8,128)S(1)} %get-tuple-element.167), channel_id=1, source_target_pairs={{0,24},{1,9},{2,26},{3,11},{4,28},{5,13},{6,30},{7,15},{8,16},{9,1... | collective-permute-start | bytes 1572872 | tf_op jit(solution)/shard_map/ppermute | solution.py:462
  133.1 15.2 %collective-permute-start.39 = (f32[2,64,8,128]{3,2,1,0:T(8,128)S(1)}, f32[2,64,8,128]{3,2,1,0:T(8,128)S(1)}, u32[]{:S(2)}, u32[]{:S(2)}) collective-permute-start(f32[2,64,8,128]{3,2,1,0:T(8,128)S(1)} %get-tuple-element.208), channel_id=1, source_target_pairs={{0,6},{1,3},{2,4},{3,1},{4,2},{5,7},{6,0},{7,5},{8,14},{9,11},{10,... | collective-permute-start | bytes 1572872 | tf_op jit(solution)/shard_map/ppermute | solution.py:462
  136.7 13.9 %collective-permute-start.33 = (f32[2,64,8,128]{3,2,1,0:T(8,128)S(1)}, f32[2,64,8,128]{3,2,1,0:T(8,128)S(1)}, u32[]{:S(2)}, u32[]{:S(2)}) collective-permute-start(f32[2,64,8,128]{3,2,1,0:T(8,128)S(1)} %get-tuple-element.196), channel_id=1, source_target_pairs={{0,96},{1,33},{2,98},{3,35},{4,100},{5,37},{6,102},{7,39},{8,104},... | collective-permute-start | bytes 1572872 | tf_op jit(solution)/shard_map/ppermute | solution.py:462
  136.8 15.0 %collective-permute-start.25 = (f32[2,64,8,128]{3,2,1,0:T(8,128)S(1)}, f32[2,64,8,128]{3,2,1,0:T(8,128)S(1)}, u32[]{:S(2)}, u32[]{:S(2)}) collective-permute-start(f32[2,64,8,128]{3,2,1,0:T(8,128)S(1)} %get-tuple-element.181), channel_id=1, source_target_pairs={{0,24},{1,9},{2,26},{3,11},{4,28},{5,13},{6,30},{7,15},{8,16},{9,1... | collective-permute-start | bytes 1572872 | tf_op jit(solution)/shard_map/ppermute | solution.py:462
  138.2 15.8 %collective-permute-start.19 = (f32[2,64,8,128]{3,2,1,0:T(8,128)S(1)}, f32[2,64,8,128]{3,2,1,0:T(8,128)S(1)}, u32[]{:S(2)}, u32[]{:S(2)}) collective-permute-start(f32[2,64,8,128]{3,2,1,0:T(8,128)S(1)} %get-tuple-element.169), channel_id=1, source_target_pairs={{0,6},{1,3},{2,4},{3,1},{4,2},{5,7},{6,0},{7,5},{8,14},{9,11},{10,... | collective-permute-start | bytes 1572872 | tf_op jit(solution)/shard_map/ppermute | solution.py:462
  (32 other events, 329.7 us)
where the time goes:
time: 161 us
  starting transfers between devices  74.3 us (46%)
  waiting for transfers between devices  52.3 us (32%)
  Pallas kernels  32.2 us (20%)
  between operations  1.72 us (1%)
    ppermute x53, starting transfers between devices, permute(): return lax.ppermute(value, 'pa', pairs)  74.3 us
    ppermute x53, waiting for transfers between devices, permute(): return lax.ppermute(value, 'pa', pairs)  52.3 us
    pallas_call x8, Pallas kernels, post(): pl.pallas_call(functools.partial(post_kernel, frame=frame), in_specs=[VME...  9.21 us
    pallas_call x3, Pallas kernels, short(): pl.pallas_call(short_kernel, grid=(count,), in_specs=[frame, frame, VMEM,...  8.11 us
    pallas_call x3, Pallas kernels, pre(): pl.pallas_call(functools.partial(pre_kernel, first=first), grid=(count,),...  6.85 us
    pallas_call x48, Pallas kernels, gather(): pl.pallas_call(kernel, in_specs=[VMEM] * 2, out_specs=[VMEM] * 2, out_sha...  3.78 us
  transfers between devices with their start and end apart: 53, of which 24 were waited for; matrix products, arithmetic and copies ran while one was open for 0% of the time, Pallas kernels for 18%

commit v1 on v0

--- a/solution.py
+++ b/solution.py
@@ -26,13 +26,13 @@
     ((0, 2, 1, 3, 4, 5), (3, 5, 4, 0, 1, 2)),
     ((2, 1, 0, 4, 5, 3), (5, 4, 3, 1, 2, 0)),
     ((1, 0, 2, 5, 3, 4), (4, 3, 5, 2, 0, 1)),
-    ((0, 2, 1, 3, 4, 5), (3, 5, 4, 0, 1, 2)),
+    ((0, 2, 4, 3, 1, 5), (3, 5, 1, 0, 4, 2)),
     ((2, 1, 0, 4, 5, 3), (5, 4, 3, 1, 2, 0)),
     ((0, 1, 2, 3, 5, 4), (3, 4, 5, 0, 2, 1)),
 )
 STEPS = len(EDGES)
 SLOTS = 64
-GROUPS = ((0, 2), (2, 2), (4, 4))
+GROUPS = ((0, 2), (2, 2), (4, 2), (6, 2))
 
 
 def recode(chip):
@@ -205,13 +205,31 @@
             out[plane, pl.ds(frame % 4 * 2, 2), :] = rows_ref[plane, frame, pl.ds(SUB - 2, 2), :]
 
 
-def short_kernel(real_ref, imag_ref, col_ref, tw_ref, z_ref):
-    z = z_ref.at[pl.program_id(0)]
-
-    @pl.loop(0, 4)
-    def _(block):
-        row = pl.multiple_of(block * SUB, SUB)
-        short_stage((real_ref.at[0], imag_ref.at[0]), row, col_ref, tw_ref, z, pl.multiple_of(row * SHORT, SUB * SHORT))
+def short_kernel(real_ref, imag_ref, col_ref, tw_ref, target_ref, source_ref, base_ref, *refs):
+    zs, (forward_ref, backward_ref, x_ref, sem) = refs[:-4], refs[-4:]
+
+    def fetch(frame, plane):
+        return pltpu.make_async_copy((real_ref, imag_ref)[plane].at[frame], x_ref.at[frame, plane], sem.at[frame, plane])
+
+    for frame in range(FRAMES):
+        for plane in range(2):
+            fetch(frame, plane).start()
+
+    matrix_kernel(target_ref, source_ref, base_ref, forward_ref, backward_ref)
+
+    for (first, count), z_ref in zip(GROUPS, zs):
+
+        @pl.loop(0, count)
+        def _(local):
+            frame = first + local
+            for plane in range(2):
+                fetch(frame, plane).wait()
+            planes, z = (x_ref.at[frame, 0], x_ref.at[frame, 1]), z_ref.at[local]
+
+            @pl.loop(0, 4)
+            def _(block):
+                row = pl.multiple_of(block * SUB, SUB)
+                short_stage(planes, row, col_ref, tw_ref, z, pl.multiple_of(row * SHORT, SUB * SHORT))
 
 
 def edge_kernel(halo_ref, col_ref, tw_ref, out_ref):
@@ -319,24 +337,12 @@
 
 
 VMEM = pl.BlockSpec(memory_space=pltpu.VMEM)
+ANY = pl.BlockSpec(memory_space=pl.ANY)
 PARAMS = pltpu.CompilerParams(vmem_limit_bytes=12 * 2**20)
 
 
 def cost(flops):
     return pl.CostEstimate(flops=flops, bytes_accessed=2**21, transcendentals=0)
-
-
-def matrices(target, source):
-    shape = jax.ShapeDtypeStruct((len(ORDERS), 2, 2 * LONG, 2 * LONG), jnp.bfloat16)
-    return pl.pallas_call(
-        matrix_kernel,
-        in_specs=[VMEM] * 3,
-        out_specs=[VMEM] * 2,
-        out_shape=[shape] * 2,
-        compiler_params=PARAMS,
-        cost_estimate=cost(10**6),
-        name="matrices",
-    )(target, source, jnp.asarray(long_matrix()))
 
 
 def in_hbm(*arrays):
@@ -347,7 +353,7 @@
     half = jax.ShapeDtypeStruct((2, SUB, N), jnp.float32)
     return pl.pallas_call(
         last_kernel,
-        in_specs=[pl.BlockSpec(memory_space=pl.ANY)] * 2,
+        in_specs=[ANY] * 2,
         out_specs=[VMEM] * 2,
         out_shape=[half] * 2,
         scratch_shapes=[pltpu.VMEM((2, FRAMES, SUB, N), jnp.float32), pltpu.SemaphoreType.DMA((2,))],
@@ -357,17 +363,19 @@
     )(*in_hbm(real, imag))
 
 
-def short(first, count, real, imag, col, tw):
-    frame = pl.BlockSpec((1, SHORT, N), lambda f: (first + f, 0, 0))
-    return pl.pallas_call(
+def short(real, imag, col, tw, target, source):
+    matrix = jax.ShapeDtypeStruct((FRAMES, 2, 2 * LONG, 2 * LONG), jnp.bfloat16)
+    *zs, forward, backward = pl.pallas_call(
         short_kernel,
-        grid=(count,),
-        in_specs=[frame, frame, VMEM, VMEM],
-        out_specs=VMEM,
-        out_shape=jax.ShapeDtypeStruct((count, 2, ROWS, LANES), jnp.float32),
-        compiler_params=pltpu.CompilerParams(vmem_limit_bytes=12 * 2**20),
+        in_specs=[ANY] * 2 + [VMEM] * 5,
+        out_specs=[VMEM] * (len(GROUPS) + 2),
+        out_shape=[jax.ShapeDtypeStruct((count, 2, ROWS, LANES), jnp.float32) for _, count in GROUPS] + [matrix] * 2,
+        scratch_shapes=[pltpu.VMEM((FRAMES, 2, SHORT, N), jnp.float32), pltpu.SemaphoreType.DMA((FRAMES, 2))],
+        compiler_params=PARAMS,
         cost_estimate=cost(10**9),
-    )(*in_hbm(real, imag), col, tw)
+        name="short",
+    )(*in_hbm(real, imag), col, tw, target, source, jnp.asarray(long_matrix()))
+    return zs, forward, backward
 
 
 def edges(halo, col, tw):
@@ -403,7 +411,6 @@
 
 WIDE = jax.ShapeDtypeStruct((2, SHORT, N), jnp.float32)
 OUT = jax.ShapeDtypeStruct((FRAMES, SHORT, N), jnp.float32)
-ANY = pl.BlockSpec(memory_space=pl.ANY)
 
 
 def post(frame, keep, got, tw, mat, before, outs):
@@ -478,13 +485,9 @@
     row = jnp.broadcast_to(row[:, None, None], (rows, SUB, LANES)).reshape(rows * SUB, LANES)
     col = jnp.asarray(column_window())
     tw = jnp.asarray(twiddles())
-    z = []
-    for first, count in GROUPS:
-        z.append(short(first, count, real, imag, col, tw))
-    forward, backward = matrices(
-        jnp.stack([targets(me, f) for f in range(frames)]),
-        jnp.stack([sources(me, f) for f in range(frames)], axis=1),
-    )
+    target = jnp.stack([targets(me, f) for f in range(frames)])
+    source = jnp.stack([sources(me, f) for f in range(frames)], axis=1)
+    z, forward, backward = short(real, imag, col, tw, target, source)
     edge = [edges(halo, col, tw) for halo in halos]
     halves = []
     for (first, count), part in zip(GROUPS, z):

time: 161 us -> 154 us (0.957)
  the two profiles are of different devices: /device:TPU:4 before, /device:TPU:0 now
where the time goes in v1:
time: 154 us
  starting transfers between devices  79.3 us (51%)
  waiting for transfers between devices  44.8 us (29%)
  Pallas kernels  27.9 us (18%)
  between operations  1.74 us (1%)
    ppermute x54, starting transfers between devices, permute(): return lax.ppermute(value, 'pa', pairs)  79.3 us
    ppermute x54, waiting for transfers between devices, permute(): return lax.ppermute(value, 'pa', pairs)  44.8 us
    pallas_call x8, Pallas kernels, post(): pl.pallas_call(functools.partial(post_kernel, frame=frame), in_specs=[VME...  9.27 us
    pallas_call x4, Pallas kernels, pre(): pl.pallas_call(functools.partial(pre_kernel, first=first), grid=(count,),...  6.87 us
    pallas_call x1, Pallas kernels, short(): pl.pallas_call(short_kernel, in_specs=[ANY] * 2 + [VMEM] * 5, out_specs=[...  5.01 us
    pallas_call x48, Pallas kernels, gather(): pl.pallas_call(kernel, in_specs=[VMEM] * 2, out_specs=[VMEM] * 2, out_sha...  3.79 us
  transfers between devices with their start and end apart: 54, of which 21 were waited for; matrix products, arithmetic and copies ran while one was open for 0% of the time, Pallas kernels for 16%

profile of v1, /device:TPU:0, one launch (start us, length us, event | category | flops | bytes accessed | tf_op | source)
XLA Modules:
  0.0 154.3 jit_solution(14697490846518483566)
XLA Ops:
  3.7 4.3 %collective-permute-start.27 = (f32[2,8,4096]{2,1,0:T(8,128)S(1)}, f32[2,8,4096]{2,1,0:T(8,128)S(1)}, u32[]{:S(2)}, u32[]{:S(2)}) collective-permute-start(f32[2,8,4096]{2,1,0:T(8,128)S(1)} %get-tuple-element.193), channel_id=1, source_target_pairs={{0,1},{1,2},{2,3},{3,4},{4,5},{5,6},{6,7},{7,8},{8,9},{9,10},{10,1... | collective-permute-start | bytes 786440 | tf_op jit(solution)/shard_map/ppermute | solution.py:469
  8.6 5.0 %short.1 = (f32[2,2,1024,128]{3,2,1,0:T(8,128)S(1)}, f32[2,2,1024,128]{3,2,1,0:T(8,128)S(1)}, f32[2,2,1024,128]{3,2,1,0:T(8,128)S(1)}, f32[2,2,1024,128]{3,2,1,0...) custom-call(f32[8,32,4096]{2,1,0:T(8,128)} %real_ref.3, ...), custom_call_target="tpu_custom_call" | custom-call | flops 1000000000 | bytes 2097152 | tf_op jit(solution)/shard_map/short/pallas_call | solution.py:368
  31.6 5.1 %collective-permute-start.2 = (f32[2,64,8,128]{3,2,1,0:T(8,128)S(1)}, f32[2,64,8,128]{3,2,1,0:T(8,128)S(1)}, u32[]{:S(2)}, u32[]{:S(2)}) collective-permute-start(f32[2,64,8,128]{3,2,1,0:T(8,128)S(1)} %get-tuple-element.141), channel_id=1, source_target_pairs={{0,32},{1,97},{2,34},{3,99},{4,36},{5,101},{6,38},{7,103},{8,40},{... | collective-permute-start | bytes 1572872 | tf_op jit(solution)/shard_map/ppermute | solution.py:469
  37.4 3.1 %collective-permute-start.49 = (f32[2,64,8,128]{3,2,1,0:T(8,128)S(1)}, f32[2,64,8,128]{3,2,1,0:T(8,128)S(1)}, u32[]{:S(2)}, u32[]{:S(2)}) collective-permute-start(f32[2,64,8,128]{3,2,1,0:T(8,128)S(1)} %get-tuple-element.238), channel_id=1, source_target_pairs={{0,8},{1,25},{2,10},{3,27},{4,12},{5,29},{6,14},{7,31},{8,0},{9,17... | collective-permute-start | bytes 1572872 | tf_op jit(solution)/shard_map/ppermute | solution.py:469
  40.7 2.2 %collective-permute-done.8 = f32[2,64,8,128]{3,2,1,0:T(8,128)S(1)} collective-permute-done((f32[2,64,8,128]{3,2,1,0:T(8,128)S(1)}, f32[2,64,8,128]{3,2,1,0:T(8,128)S(1)}, u32[]{:S(2)}, u32[]{:S(2)}) %collective-permute-start.8) | collective-permute-done | bytes 524320 | tf_op jit(solution)/shard_map/ppermute | solution.py:469
  42.8 5.0 %collective-permute-start.43 = (f32[2,64,8,128]{3,2,1,0:T(8,128)S(1)}, f32[2,64,8,128]{3,2,1,0:T(8,128)S(1)}, u32[]{:S(2)}, u32[]{:S(2)}) collective-permute-start(f32[2,64,8,128]{3,2,1,0:T(8,128)S(1)} %get-tuple-element.226), channel_id=1, source_target_pairs={{0,32},{1,97},{2,34},{3,99},{4,36},{5,101},{6,38},{7,103},{8,40},{... | collective-permute-start | bytes 1572872 | tf_op jit(solution)/shard_map/ppermute | solution.py:469
  51.7 3.3 %collective-permute-done.43 = f32[2,64,8,128]{3,2,1,0:T(8,128)S(1)} collective-permute-done((f32[2,64,8,128]{3,2,1,0:T(8,128)S(1)}, f32[2,64,8,128]{3,2,1,0:T(8,128)S(1)}, u32[]{:S(2)}, u32[]{:S(2)}) %collective-permute-start.43) | collective-permute-done | bytes 524320 | tf_op jit(solution)/shard_map/ppermute | solution.py:469
  57.7 5.3 %collective-permute-done.9 = f32[2,64,8,128]{3,2,1,0:T(8,128)S(1)} collective-permute-done((f32[2,64,8,128]{3,2,1,0:T(8,128)S(1)}, f32[2,64,8,128]{3,2,1,0:T(8,128)S(1)}, u32[]{:S(2)}, u32[]{:S(2)}) %collective-permute-start.9) | collective-permute-done | bytes 524320 | tf_op jit(solution)/shard_map/ppermute | solution.py:469
  65.2 3.5 %collective-permute-done.3 = f32[2,64,8,128]{3,2,1,0:T(8,128)S(1)} collective-permute-done((f32[2,64,8,128]{3,2,1,0:T(8,128)S(1)}, f32[2,64,8,128]{3,2,1,0:T(8,128)S(1)}, u32[]{:S(2)}, u32[]{:S(2)}) %collective-permute-start.3) | collective-permute-done | bytes 524320 | tf_op jit(solution)/shard_map/ppermute | solution.py:469
  74.3 3.5 %collective-permute-done.37 = f32[2,64,8,128]{3,2,1,0:T(8,128)S(1)} collective-permute-done((f32[2,64,8,128]{3,2,1,0:T(8,128)S(1)}, f32[2,64,8,128]{3,2,1,0:T(8,128)S(1)}, u32[]{:S(2)}, u32[]{:S(2)}) %collective-permute-start.37) | collective-permute-done | bytes 524320 | tf_op jit(solution)/shard_map/ppermute | solution.py:469
  81.3 2.3 %collective-permute-done.10 = f32[2,64,8,128]{3,2,1,0:T(8,128)S(1)} collective-permute-done((f32[2,64,8,128]{3,2,1,0:T(8,128)S(1)}, f32[2,64,8,128]{3,2,1,0:T(8,128)S(1)}, u32[]{:S(2)}, u32[]{:S(2)}) %collective-permute-start.10) | collective-permute-done | bytes 524320 | tf_op jit(solution)/shard_map/ppermute | solution.py:469
  85.5 2.2 %collective-permute-start.38 = (f32[2,64,8,128]{3,2,1,0:T(8,128)S(1)}, f32[2,64,8,128]{3,2,1,0:T(8,128)S(1)}, u32[]{:S(2)}, u32[]{:S(2)}) collective-permute-start(f32[2,64,8,128]{3,2,1,0:T(8,128)S(1)} %get-tuple-element.215), channel_id=1, source_target_pairs={{0,96},{1,33},{2,98},{3,35},{4,100},{5,37},{6,102},{7,39},{8,104},... | collective-permute-start | bytes 1572872 | tf_op jit(solution)/shard_map/ppermute | solution.py:469
  87.8 2.6 %collective-permute-start.32 = (f32[2,64,8,128]{3,2,1,0:T(8,128)S(1)}, f32[2,64,8,128]{3,2,1,0:T(8,128)S(1)}, u32[]{:S(2)}, u32[]{:S(2)}) collective-permute-start(f32[2,64,8,128]{3,2,1,0:T(8,128)S(1)} %get-tuple-element.203), channel_id=1, source_target_pairs={{0,24},{1,9},{2,26},{3,11},{4,28},{5,13},{6,30},{7,15},{8,16},{9,1... | collective-permute-start | bytes 1572872 | tf_op jit(solution)/shard_map/ppermute | solution.py:469
  91.3 2.5 %collective-permute-done.51 = f32[2,64,8,128]{3,2,1,0:T(8,128)S(1)} collective-permute-done((f32[2,64,8,128]{3,2,1,0:T(8,128)S(1)}, f32[2,64,8,128]{3,2,1,0:T(8,128)S(1)}, u32[]{:S(2)}, u32[]{:S(2)}) %collective-permute-start.51) | collective-permute-done | bytes 524320 | tf_op jit(solution)/shard_map/ppermute | solution.py:469
  93.9 2.1 %collective-permute-start.5 = (f32[2,64,8,128]{3,2,1,0:T(8,128)S(1)}, f32[2,64,8,128]{3,2,1,0:T(8,128)S(1)}, u32[]{:S(2)}, u32[]{:S(2)}) collective-permute-start(f32[2,64,8,128]{3,2,1,0:T(8,128)S(1)} %get-tuple-element.147), channel_id=1, source_target_pairs={{0,96},{1,33},{2,98},{3,35},{4,100},{5,37},{6,102},{7,39},{8,104},... | collective-permute-start | bytes 1572872 | tf_op jit(solution)/shard_map/ppermute | solution.py:469
  96.1 2.2 %collective-permute-start.24 = (f32[2,64,8,128]{3,2,1,0:T(8,128)S(1)}, f32[2,64,8,128]{3,2,1,0:T(8,128)S(1)}, u32[]{:S(2)}, u32[]{:S(2)}) collective-permute-start(f32[2,64,8,128]{3,2,1,0:T(8,128)S(1)} %get-tuple-element.187), channel_id=1, source_target_pairs={{0,6},{1,3},{2,4},{3,1},{4,2},{5,7},{6,0},{7,5},{8,14},{9,11},{10,... | collective-permute-start | bytes 1572872 | tf_op jit(solution)/shard_map/ppermute | solution.py:469
  100.9 4.2 %collective-permute-done.11 = f32[2,64,8,128]{3,2,1,0:T(8,128)S(1)} collective-permute-done((f32[2,64,8,128]{3,2,1,0:T(8,128)S(1)}, f32[2,64,8,128]{3,2,1,0:T(8,128)S(1)}, u32[]{:S(2)}, u32[]{:S(2)}) %collective-permute-start.11) | collective-permute-done | bytes 524320 | tf_op jit(solution)/shard_map/ppermute | solution.py:469
  105.1 2.1 %collective-permute-start.46 = (f32[2,64,8,128]{3,2,1,0:T(8,128)S(1)}, f32[2,64,8,128]{3,2,1,0:T(8,128)S(1)}, u32[]{:S(2)}, u32[]{:S(2)}) collective-permute-start(f32[2,64,8,128]{3,2,1,0:T(8,128)S(1)} %get-tuple-element.232), channel_id=1, source_target_pairs={{0,96},{1,33},{2,98},{3,35},{4,100},{5,37},{6,102},{7,39},{8,104},... | collective-permute-start | bytes 1572872 | tf_op jit(solution)/shard_map/ppermute | solution.py:469
  107.3 2.1 %collective-permute-start.39 = (f32[2,64,8,128]{3,2,1,0:T(8,128)S(1)}, f32[2,64,8,128]{3,2,1,0:T(8,128)S(1)}, u32[]{:S(2)}, u32[]{:S(2)}) collective-permute-start(f32[2,64,8,128]{3,2,1,0:T(8,128)S(1)} %get-tuple-element.217), channel_id=1, source_target_pairs={{0,24},{1,9},{2,26},{3,11},{4,28},{5,13},{6,30},{7,15},{8,16},{9,1... | collective-permute-start | bytes 1572872 | tf_op jit(solution)/shard_map/ppermute | solution.py:469
  115.5 2.1 %collective-permute-start.25 = (f32[2,64,8,128]{3,2,1,0:T(8,128)S(1)}, f32[2,64,8,128]{3,2,1,0:T(8,128)S(1)}, u32[]{:S(2)}, u32[]{:S(2)}) collective-permute-start(f32[2,64,8,128]{3,2,1,0:T(8,128)S(1)} %get-tuple-element.189), channel_id=1, source_target_pairs={{0,96},{1,33},{2,98},{3,35},{4,100},{5,37},{6,102},{7,39},{8,104},... | collective-permute-start | bytes 1572872 | tf_op jit(solution)/shard_map/ppermute | solution.py:469
  121.2 4.4 %collective-permute-done.12 = f32[2,64,8,128]{3,2,1,0:T(8,128)S(1)} collective-permute-done((f32[2,64,8,128]{3,2,1,0:T(8,128)S(1)}, f32[2,64,8,128]{3,2,1,0:T(8,128)S(1)}, u32[]{:S(2)}, u32[]{:S(2)}) %collective-permute-start.12) | collective-permute-done | bytes 524320 | tf_op jit(solution)/shard_map/ppermute | solution.py:469
  126.9 4.3 %collective-permute-done.6 = f32[2,64,8,128]{3,2,1,0:T(8,128)S(1)} collective-permute-done((f32[2,64,8,128]{3,2,1,0:T(8,128)S(1)}, f32[2,64,8,128]{3,2,1,0:T(8,128)S(1)}, u32[]{:S(2)}, u32[]{:S(2)}) %collective-permute-start.6) | collective-permute-done | bytes 524320 | tf_op jit(solution)/shard_map/ppermute | solution.py:469
  134.9 2.4 %collective-permute-start.20 = (f32[2,64,8,128]{3,2,1,0:T(8,128)S(1)}, f32[2,64,8,128]{3,2,1,0:T(8,128)S(1)}, u32[]{:S(2)}, u32[]{:S(2)}) collective-permute-start(f32[2,64,8,128]{3,2,1,0:T(8,128)S(1)} %get-tuple-element.179), channel_id=1, source_target_pairs={{0,6},{1,3},{2,4},{3,1},{4,2},{5,7},{6,0},{7,5},{8,14},{9,11},{10,... | collective-permute-start | bytes 1572872 | tf_op jit(solution)/shard_map/ppermute | solution.py:469
  137.5 2.2 %collective-permute-start.13 = (f32[2,64,8,128]{3,2,1,0:T(8,128)S(1)}, f32[2,64,8,128]{3,2,1,0:T(8,128)S(1)}, u32[]{:S(2)}, u32[]{:S(2)}) collective-permute-start(f32[2,64,8,128]{3,2,1,0:T(8,128)S(1)} %get-tuple-element.164), channel_id=1, source_target_pairs={{0,96},{1,33},{2,98},{3,35},{4,100},{5,37},{6,102},{7,39},{8,104},... | collective-permute-start | bytes 1572872 | tf_op jit(solution)/shard_map/ppermute | solution.py:469
  (168 shorter events, 74.5 us)
Async XLA Ops:
  2.4 15.6 %collective-permute-start = (f32[2,8,4096]{2,1,0:T(8,128)S(1)}, f32[2,8,4096]{2,1,0:T(8,128)S(1)}, u32[]{:S(2)}, u32[]{:S(2)}) collective-permute-start(f32[2,8,4096]{2,1,0:T(8,128)S(1)} %get-tuple-element.136), channel_id=1, source_target_pairs={{0,1},{1,2},{2,3},{3,4},{4,5},{5,6},{6,7},{7,8},{8,9},{9,10},{10,1... | collective-permute-start | bytes 786440 | tf_op jit(solution)/shard_map/ppermute | solution.py:469
  30.2 12.7 %collective-permute-start.8 = (f32[2,64,8,128]{3,2,1,0:T(8,128)S(1)}, f32[2,64,8,128]{3,2,1,0:T(8,128)S(1)}, u32[]{:S(2)}, u32[]{:S(2)}) collective-permute-start(f32[2,64,8,128]{3,2,1,0:T(8,128)S(1)} %get-tuple-element.154), channel_id=1, source_target_pairs={{0,2},{1,7},{2,0},{3,5},{4,6},{5,3},{6,4},{7,1},{8,10},{9,15},{10,... | collective-permute-start | bytes 1572872 | tf_op jit(solution)/shard_map/ppermute | solution.py:469
  31.6 16.4 %collective-permute-start.2 = (f32[2,64,8,128]{3,2,1,0:T(8,128)S(1)}, f32[2,64,8,128]{3,2,1,0:T(8,128)S(1)}, u32[]{:S(2)}, u32[]{:S(2)}) collective-permute-start(f32[2,64,8,128]{3,2,1,0:T(8,128)S(1)} %get-tuple-element.141), channel_id=1, source_target_pairs={{0,32},{1,97},{2,34},{3,99},{4,36},{5,101},{6,38},{7,103},{8,40},{... | collective-permute-start | bytes 1572872 | tf_op jit(solution)/shard_map/ppermute | solution.py:469
  37.4 14.2 %collective-permute-start.49 = (f32[2,64,8,128]{3,2,1,0:T(8,128)S(1)}, f32[2,64,8,128]{3,2,1,0:T(8,128)S(1)}, u32[]{:S(2)}, u32[]{:S(2)}) collective-permute-start(f32[2,64,8,128]{3,2,1,0:T(8,128)S(1)} %get-tuple-element.238), channel_id=1, source_target_pairs={{0,8},{1,25},{2,10},{3,27},{4,12},{5,29},{6,14},{7,31},{8,0},{9,17... | collective-permute-start | bytes 1572872 | tf_op jit(solution)/shard_map/ppermute | solution.py:469
  49.4 13.7 %collective-permute-start.9 = (f32[2,64,8,128]{3,2,1,0:T(8,128)S(1)}, f32[2,64,8,128]{3,2,1,0:T(8,128)S(1)}, u32[]{:S(2)}, u32[]{:S(2)}) collective-permute-start(f32[2,64,8,128]{3,2,1,0:T(8,128)S(1)} %get-tuple-element.156), channel_id=1, source_target_pairs={{0,8},{1,25},{2,10},{3,27},{4,12},{5,29},{6,14},{7,31},{8,0},{9,17... | collective-permute-start | bytes 1572872 | tf_op jit(solution)/shard_map/ppermute | solution.py:469
  51.6 17.1 %collective-permute-start.3 = (f32[2,64,8,128]{3,2,1,0:T(8,128)S(1)}, f32[2,64,8,128]{3,2,1,0:T(8,128)S(1)}, u32[]{:S(2)}, u32[]{:S(2)}) collective-permute-start(f32[2,64,8,128]{3,2,1,0:T(8,128)S(1)} %get-tuple-element.143), channel_id=1, source_target_pairs={{0,8},{1,25},{2,10},{3,27},{4,12},{5,29},{6,14},{7,31},{8,0},{9,17... | collective-permute-start | bytes 1572872 | tf_op jit(solution)/shard_map/ppermute | solution.py:469
  55.0 13.8 %collective-permute-start.22 = (f32[2,64,8,128]{3,2,1,0:T(8,128)S(1)}, f32[2,64,8,128]{3,2,1,0:T(8,128)S(1)}, u32[]{:S(2)}, u32[]{:S(2)}) collective-permute-start(f32[2,64,8,128]{3,2,1,0:T(8,128)S(1)} %get-tuple-element.183), channel_id=1, source_target_pairs={{0,32},{1,97},{2,34},{3,99},{4,36},{5,101},{6,38},{7,103},{8,40},{... | collective-permute-start | bytes 1572872 | tf_op jit(solution)/shard_map/ppermute | solution.py:469
  57.5 13.6 %collective-permute-start.50 = (f32[2,64,8,128]{3,2,1,0:T(8,128)S(1)}, f32[2,64,8,128]{3,2,1,0:T(8,128)S(1)}, u32[]{:S(2)}, u32[]{:S(2)}) collective-permute-start(f32[2,64,8,128]{3,2,1,0:T(8,128)S(1)} %get-tuple-element.240), channel_id=1, source_target_pairs={{0,32},{1,97},{2,34},{3,99},{4,36},{5,101},{6,38},{7,103},{8,40},{... | collective-permute-start | bytes 1572872 | tf_op jit(solution)/shard_map/ppermute | solution.py:469
  69.9 13.7 %collective-permute-start.10 = (f32[2,64,8,128]{3,2,1,0:T(8,128)S(1)}, f32[2,64,8,128]{3,2,1,0:T(8,128)S(1)}, u32[]{:S(2)}, u32[]{:S(2)}) collective-permute-start(f32[2,64,8,128]{3,2,1,0:T(8,128)S(1)} %get-tuple-element.158), channel_id=1, source_target_pairs={{0,32},{1,97},{2,34},{3,99},{4,36},{5,101},{6,38},{7,103},{8,40},{... | collective-permute-start | bytes 1572872 | tf_op jit(solution)/shard_map/ppermute | solution.py:469
  71.2 14.3 %collective-permute-start.4 = (f32[2,64,8,128]{3,2,1,0:T(8,128)S(1)}, f32[2,64,8,128]{3,2,1,0:T(8,128)S(1)}, u32[]{:S(2)}, u32[]{:S(2)}) collective-permute-start(f32[2,64,8,128]{3,2,1,0:T(8,128)S(1)} %get-tuple-element.145), channel_id=1, source_target_pairs={{0,2},{1,7},{2,0},{3,5},{4,6},{5,3},{6,4},{7,1},{8,10},{9,15},{10,... | collective-permute-start | bytes 1572872 | tf_op jit(solution)/shard_map/ppermute | solution.py:469
  73.4 14.4 %collective-permute-start.23 = (f32[2,64,8,128]{3,2,1,0:T(8,128)S(1)}, f32[2,64,8,128]{3,2,1,0:T(8,128)S(1)}, u32[]{:S(2)}, u32[]{:S(2)}) collective-permute-start(f32[2,64,8,128]{3,2,1,0:T(8,128)S(1)} %get-tuple-element.185), channel_id=1, source_target_pairs={{0,2},{1,7},{2,0},{3,5},{4,6},{5,3},{6,4},{7,1},{8,10},{9,15},{10,... | collective-permute-start | bytes 1572872 | tf_op jit(solution)/shard_map/ppermute | solution.py:469
  80.0 13.9 %collective-permute-start.51 = (f32[2,64,8,128]{3,2,1,0:T(8,128)S(1)}, f32[2,64,8,128]{3,2,1,0:T(8,128)S(1)}, u32[]{:S(2)}, u32[]{:S(2)}) collective-permute-start(f32[2,64,8,128]{3,2,1,0:T(8,128)S(1)} %get-tuple-element.242), channel_id=1, source_target_pairs={{0,24},{1,9},{2,26},{3,11},{4,28},{5,13},{6,30},{7,15},{8,16},{9,1... | collective-permute-start | bytes 1572872 | tf_op jit(solution)/shard_map/ppermute | solution.py:469
  85.5 12.8 %collective-permute-start.38 = (f32[2,64,8,128]{3,2,1,0:T(8,128)S(1)}, f32[2,64,8,128]{3,2,1,0:T(8,128)S(1)}, u32[]{:S(2)}, u32[]{:S(2)}) collective-permute-start(f32[2,64,8,128]{3,2,1,0:T(8,128)S(1)} %get-tuple-element.215), channel_id=1, source_target_pairs={{0,96},{1,33},{2,98},{3,35},{4,100},{5,37},{6,102},{7,39},{8,104},... | collective-permute-start | bytes 1572872 | tf_op jit(solution)/shard_map/ppermute | solution.py:469
  90.5 14.6 %collective-permute-start.11 = (f32[2,64,8,128]{3,2,1,0:T(8,128)S(1)}, f32[2,64,8,128]{3,2,1,0:T(8,128)S(1)}, u32[]{:S(2)}, u32[]{:S(2)}) collective-permute-start(f32[2,64,8,128]{3,2,1,0:T(8,128)S(1)} %get-tuple-element.160), channel_id=1, source_target_pairs={{0,24},{1,9},{2,26},{3,11},{4,28},{5,13},{6,30},{7,15},{8,16},{9,1... | collective-permute-start | bytes 1572872 | tf_op jit(solution)/shard_map/ppermute | solution.py:469
  93.9 13.4 %collective-permute-start.5 = (f32[2,64,8,128]{3,2,1,0:T(8,128)S(1)}, f32[2,64,8,128]{3,2,1,0:T(8,128)S(1)}, u32[]{:S(2)}, u32[]{:S(2)}) collective-permute-start(f32[2,64,8,128]{3,2,1,0:T(8,128)S(1)} %get-tuple-element.147), channel_id=1, source_target_pairs={{0,96},{1,33},{2,98},{3,35},{4,100},{5,37},{6,102},{7,39},{8,104},... | collective-permute-start | bytes 1572872 | tf_op jit(solution)/shard_map/ppermute | solution.py:469
  96.1 13.4 %collective-permute-start.24 = (f32[2,64,8,128]{3,2,1,0:T(8,128)S(1)}, f32[2,64,8,128]{3,2,1,0:T(8,128)S(1)}, u32[]{:S(2)}, u32[]{:S(2)}) collective-permute-start(f32[2,64,8,128]{3,2,1,0:T(8,128)S(1)} %get-tuple-element.187), channel_id=1, source_target_pairs={{0,6},{1,3},{2,4},{3,1},{4,2},{5,7},{6,0},{7,5},{8,14},{9,11},{10,... | collective-permute-start | bytes 1572872 | tf_op jit(solution)/shard_map/ppermute | solution.py:469
  98.4 13.1 %collective-permute-start.18 = (f32[2,64,8,128]{3,2,1,0:T(8,128)S(1)}, f32[2,64,8,128]{3,2,1,0:T(8,128)S(1)}, u32[]{:S(2)}, u32[]{:S(2)}) collective-permute-start(f32[2,64,8,128]{3,2,1,0:T(8,128)S(1)} %get-tuple-element.175), channel_id=1, source_target_pairs={{0,96},{1,33},{2,98},{3,35},{4,100},{5,37},{6,102},{7,39},{8,104},... | collective-permute-start | bytes 1572872 | tf_op jit(solution)/shard_map/ppermute | solution.py:469
  99.5 13.5 %collective-permute-start.52 = (f32[2,64,8,128]{3,2,1,0:T(8,128)S(1)}, f32[2,64,8,128]{3,2,1,0:T(8,128)S(1)}, u32[]{:S(2)}, u32[]{:S(2)}) collective-permute-start(f32[2,64,8,128]{3,2,1,0:T(8,128)S(1)} %get-tuple-element.244), channel_id=1, source_target_pairs={{0,6},{1,3},{2,4},{3,1},{4,2},{5,7},{6,0},{7,5},{8,14},{9,11},{10,... | collective-permute-start | bytes 1572872 | tf_op jit(solution)/shard_map/ppermute | solution.py:469
  111.5 14.0 %collective-permute-start.12 = (f32[2,64,8,128]{3,2,1,0:T(8,128)S(1)}, f32[2,64,8,128]{3,2,1,0:T(8,128)S(1)}, u32[]{:S(2)}, u32[]{:S(2)}) collective-permute-start(f32[2,64,8,128]{3,2,1,0:T(8,128)S(1)} %get-tuple-element.162), channel_id=1, source_target_pairs={{0,6},{1,3},{2,4},{3,1},{4,2},{5,7},{6,0},{7,5},{8,14},{9,11},{10,... | collective-permute-start | bytes 1572872 | tf_op jit(solution)/shard_map/ppermute | solution.py:469
  113.0 18.1 %collective-permute-start.6 = (f32[2,64,8,128]{3,2,1,0:T(8,128)S(1)}, f32[2,64,8,128]{3,2,1,0:T(8,128)S(1)}, u32[]{:S(2)}, u32[]{:S(2)}) collective-permute-start(f32[2,64,8,128]{3,2,1,0:T(8,128)S(1)} %get-tuple-element.149), channel_id=1, source_target_pairs={{0,6},{1,3},{2,4},{3,1},{4,2},{5,7},{6,0},{7,5},{8,14},{9,11},{10,... | collective-permute-start | bytes 1572872 | tf_op jit(solution)/shard_map/ppermute | solution.py:469
  115.5 17.6 %collective-permute-start.25 = (f32[2,64,8,128]{3,2,1,0:T(8,128)S(1)}, f32[2,64,8,128]{3,2,1,0:T(8,128)S(1)}, u32[]{:S(2)}, u32[]{:S(2)}) collective-permute-start(f32[2,64,8,128]{3,2,1,0:T(8,128)S(1)} %get-tuple-element.189), channel_id=1, source_target_pairs={{0,96},{1,33},{2,98},{3,35},{4,100},{5,37},{6,102},{7,39},{8,104},... | collective-permute-start | bytes 1572872 | tf_op jit(solution)/shard_map/ppermute | solution.py:469
  117.8 16.7 %collective-permute-start.19 = (f32[2,64,8,128]{3,2,1,0:T(8,128)S(1)}, f32[2,64,8,128]{3,2,1,0:T(8,128)S(1)}, u32[]{:S(2)}, u32[]{:S(2)}) collective-permute-start(f32[2,64,8,128]{3,2,1,0:T(8,128)S(1)} %get-tuple-element.177), channel_id=1, source_target_pairs={{0,8},{1,25},{2,10},{3,27},{4,12},{5,29},{6,14},{7,31},{8,0},{9,17... | collective-permute-start | bytes 1572872 | tf_op jit(solution)/shard_map/ppermute | solution.py:469
  119.9 15.0 %collective-permute-start.53 = (f32[2,64,8,128]{3,2,1,0:T(8,128)S(1)}, f32[2,64,8,128]{3,2,1,0:T(8,128)S(1)}, u32[]{:S(2)}, u32[]{:S(2)}) collective-permute-start(f32[2,64,8,128]{3,2,1,0:T(8,128)S(1)} %get-tuple-element.246), channel_id=1, source_target_pairs={{0,96},{1,33},{2,98},{3,35},{4,100},{5,37},{6,102},{7,39},{8,104},... | collective-permute-start | bytes 1572872 | tf_op jit(solution)/shard_map/ppermute | solution.py:469
  134.9 12.9 %collective-permute-start.20 = (f32[2,64,8,128]{3,2,1,0:T(8,128)S(1)}, f32[2,64,8,128]{3,2,1,0:T(8,128)S(1)}, u32[]{:S(2)}, u32[]{:S(2)}) collective-permute-start(f32[2,64,8,128]{3,2,1,0:T(8,128)S(1)} %get-tuple-element.179), channel_id=1, source_target_pairs={{0,6},{1,3},{2,4},{3,1},{4,2},{5,7},{6,0},{7,5},{8,14},{9,11},{10,... | collective-permute-start | bytes 1572872 | tf_op jit(solution)/shard_map/ppermute | solution.py:469
  (33 other events, 342.9 us)

commit v2 on v1

--- a/solution.py
+++ b/solution.py
@@ -21,18 +21,22 @@
 
 EDGES = (4, 2, 0, 5, 3, 1)
 ORDERS = (
-    ((2, 1, 0, 4, 5, 3), (5, 4, 3, 1, 2, 0)),
-    ((1, 0, 2, 5, 3, 4), (4, 3, 5, 2, 0, 1)),
-    ((0, 2, 1, 3, 4, 5), (3, 5, 4, 0, 1, 2)),
-    ((2, 1, 0, 4, 5, 3), (5, 4, 3, 1, 2, 0)),
-    ((1, 0, 2, 5, 3, 4), (4, 3, 5, 2, 0, 1)),
-    ((0, 2, 4, 3, 1, 5), (3, 5, 1, 0, 4, 2)),
-    ((2, 1, 0, 4, 5, 3), (5, 4, 3, 1, 2, 0)),
-    ((0, 1, 2, 3, 5, 4), (3, 4, 5, 0, 2, 1)),
+    ((0, 2, 3, 4, 1, 5), (3, 5, 0, 1, 4, 2)),
+    ((1, 3, 4, 5, 2, 0), (4, 0, 1, 2, 5, 3)),
+    ((2, 1, 3, 4, 5, 0), (5, 4, 0, 1, 2, 3)),
+    ((1, 2, 0, 3, 4, 5), (4, 5, 3, 0, 1, 2)),
+    ((3, 5, 2, 0, 4, 1), (0, 2, 5, 3, 1, 4)),
+    ((2, 0, 3, 4, 1, 5), (5, 3, 0, 1, 4, 2)),
+    ((1, 4, 2, 3, 5, 0), (4, 1, 5, 0, 2, 3)),
+    ((4, 5, 3, 0, 1, 2), (1, 2, 0, 3, 4, 5)),
 )
 STEPS = len(EDGES)
 SLOTS = 64
 GROUPS = ((0, 2), (2, 2), (4, 2), (6, 2))
+
+
+LATE = (0, 1, 2, 3)
+CORES = [(d, d ^ 1) for d in range(2 * SLOTS)]
 
 
 def recode(chip):
@@ -52,21 +56,24 @@
     return pairs
 
 
-def peer(me, frame, core_bit, steps):
-    core = me % 2 ^ core_bit
+def peer(me, frame, core, traveller, steps):
     masks = [sum(bit << edge for bit, edge in zip(steps, edges_of(frame, c))) for c in range(2)]
-    return recode(recode(me // 2) ^ jnp.where(core == 0, *masks)) * 2 + core
+    return recode(recode(me // 2) ^ jnp.where(traveller == 0, *masks)) * 2 + core
 
 
 def targets(me, frame):
     slot = jnp.arange(2 * SLOTS, dtype=jnp.int32)
-    return peer(me, frame, slot >> STEPS, [slot >> (STEPS - 1 - k) & 1 for k in range(STEPS)])
+    core = me % 2 ^ slot >> STEPS
+    steps = [slot >> (STEPS - 1 - k) & 1 for k in range(STEPS)]
+    return peer(me, frame, core, me % 2 if frame in LATE else core, steps)
 
 
 def sources(me, frame):
     slot = jnp.arange(2 * SLOTS, dtype=jnp.int32)
-    masks = [sum((slot >> (k + 1) & 1) << edge for k, edge in enumerate(edges_of(frame, c))) for c in range(2)]
-    return recode(recode(me // 2) ^ jnp.where(me % 2 == 0, *masks)) * 2 + (me % 2 ^ slot & 1)
+    if frame in LATE:
+        core = me % 2 ^ slot >> STEPS
+        return peer(me, frame, core, core, [slot >> k & 1 for k in range(STEPS)])
+    return peer(me, frame, me % 2 ^ slot & 1, me % 2, [slot >> (k + 1) & 1 for k in range(STEPS)])
 
 
 def hamming(index):
@@ -474,6 +481,9 @@
         keep, send = gather(step, *halves)
         got = permute(send, edge_pairs(frame, step))
         halves = (keep[None], 0), (got[None], 0)
+    if frame in LATE:
+        keep, send = gather(STEPS - 1, *halves)
+        got = permute(send, CORES)
     return keep, got
 
 
@@ -492,8 +502,9 @@
     halves = []
     for (first, count), part in zip(GROUPS, z):
         keep, send = pre(first, count, row, part, edge[first // 4], forward)
-        got = permute(send, [(i, i ^ 1) for i in range(2 * SLOTS)])
-        halves += [((keep, i), (got, i)) for i in range(count)]
+        if first not in LATE:
+            send = permute(send, CORES)
+        halves += [((keep, i), (send, i)) for i in range(count)]
     ends = [exchange(frame, halves[frame]) for frame in range(frames)]
     wide, outs = None, ()
     for frame in range(frames):

time: 154 us -> 192 us (1.25)
  the two profiles are of different devices: /device:TPU:0 before, /device:TPU:1 now
where the time goes in v2:
time: 192 us
  waiting for transfers between devices  81.4 us (42%)
  starting transfers between devices  79.6 us (41%)
  Pallas kernels  28.2 us (15%)
    ppermute x56, waiting for transfers between devices, permute(): return lax.ppermute(value, 'pa', pairs)  81.4 us
    ppermute x56, starting transfers between devices, permute(): return lax.ppermute(value, 'pa', pairs)  79.6 us
    pallas_call x8, Pallas kernels, post(): pl.pallas_call(functools.partial(post_kernel, frame=frame), in_specs=[VME...  9.27 us
    pallas_call x4, Pallas kernels, pre(): pl.pallas_call(functools.partial(pre_kernel, first=first), grid=(count,),...  6.87 us
    pallas_call x1, Pallas kernels, short(): pl.pallas_call(short_kernel, in_specs=[ANY] * 2 + [VMEM] * 5, out_specs=[...  5.01 us
    pallas_call x52, Pallas kernels, gather(): pl.pallas_call(kernel, in_specs=[VMEM] * 2, out_specs=[VMEM] * 2, out_sha...  4.09 us
  transfers between devices with their start and end apart: 56, of which 28 were waited for; matrix products, arithmetic and copies ran while one was open for 0% of the time, Pallas kernels for 12%

profile of v2, /device:TPU:1, one launch (start us, length us, event | category | flops | bytes accessed | tf_op | source)
XLA Modules:
  0.0 191.7 jit_solution(4326008815989209230)
XLA Ops:
  2.4 4.6 %collective-permute-start.27 = (f32[2,8,4096]{2,1,0:T(8,128)S(1)}, f32[2,8,4096]{2,1,0:T(8,128)S(1)}, u32[]{:S(2)}, u32[]{:S(2)}) collective-permute-start(f32[2,8,4096]{2,1,0:T(8,128)S(1)} %get-tuple-element.201), channel_id=1, source_target_pairs={{0,1},{1,2},{2,3},{3,4},{4,5},{5,6},{6,7},{7,8},{8,9},{9,10},{10,1... | collective-permute-start | bytes 786440 | tf_op jit(solution)/shard_map/ppermute | solution.py:476
  7.6 5.0 %short.1 = (f32[2,2,1024,128]{3,2,1,0:T(8,128)S(1)}, f32[2,2,1024,128]{3,2,1,0:T(8,128)S(1)}, f32[2,2,1024,128]{3,2,1,0:T(8,128)S(1)}, f32[2,2,1024,128]{3,2,1,0...) custom-call(f32[8,32,4096]{2,1,0:T(8,128)} %real_ref.3, ...), custom_call_target="tpu_custom_call" | custom-call | flops 1000000000 | bytes 2097152 | tf_op jit(solution)/shard_map/short/pallas_call | solution.py:375
  19.3 3.8 %collective-permute-start.42 = (f32[2,64,8,128]{3,2,1,0:T(8,128)S(1)}, f32[2,64,8,128]{3,2,1,0:T(8,128)S(1)}, u32[]{:S(2)}, u32[]{:S(2)}) collective-permute-start(f32[2,64,8,128]{3,2,1,0:T(8,128)S(1)} %get-tuple-element.236), channel_id=1, source_target_pairs={{0,8},{1,25},{2,10},{3,27},{4,12},{5,29},{6,14},{7,31},{8,0},{9,17... | collective-permute-start | bytes 1572872 | tf_op jit(solution)/shard_map/ppermute | solution.py:476
  24.9 2.9 %collective-permute-start.35 = (f32[2,64,8,128]{3,2,1,0:T(8,128)S(1)}, f32[2,64,8,128]{3,2,1,0:T(8,128)S(1)}, u32[]{:S(2)}, u32[]{:S(2)}) collective-permute-start(f32[2,64,8,128]{3,2,1,0:T(8,128)S(1)} %get-tuple-element.219), channel_id=1, source_target_pairs={{0,2},{1,7},{2,0},{3,5},{4,6},{5,3},{6,4},{7,1},{8,10},{9,15},{10,... | collective-permute-start | bytes 1572872 | tf_op jit(solution)/shard_map/ppermute | solution.py:476
  34.4 2.6 %collective-permute-start.43 = (f32[2,64,8,128]{3,2,1,0:T(8,128)S(1)}, f32[2,64,8,128]{3,2,1,0:T(8,128)S(1)}, u32[]{:S(2)}, u32[]{:S(2)}) collective-permute-start(f32[2,64,8,128]{3,2,1,0:T(8,128)S(1)} %get-tuple-element.238), channel_id=1, source_target_pairs={{0,96},{1,33},{2,98},{3,35},{4,100},{5,37},{6,102},{7,39},{8,104},... | collective-permute-start | bytes 1572872 | tf_op jit(solution)/shard_map/ppermute | solution.py:476
  40.3 2.7 %collective-permute-start.29 = (f32[2,64,8,128]{3,2,1,0:T(8,128)S(1)}, f32[2,64,8,128]{3,2,1,0:T(8,128)S(1)}, u32[]{:S(2)}, u32[]{:S(2)}) collective-permute-start(f32[2,64,8,128]{3,2,1,0:T(8,128)S(1)} %get-tuple-element.207), channel_id=1, source_target_pairs={{0,2},{1,7},{2,0},{3,5},{4,6},{5,3},{6,4},{7,1},{8,10},{9,15},{10,... | collective-permute-start | bytes 1572872 | tf_op jit(solution)/shard_map/ppermute | solution.py:476
  46.6 3.0 %collective-permute-done.29 = f32[2,64,8,128]{3,2,1,0:T(8,128)S(1)} collective-permute-done((f32[2,64,8,128]{3,2,1,0:T(8,128)S(1)}, f32[2,64,8,128]{3,2,1,0:T(8,128)S(1)}, u32[]{:S(2)}, u32[]{:S(2)}) %collective-permute-start.29) | collective-permute-done | bytes 524320 | tf_op jit(solution)/shard_map/ppermute | solution.py:476
  57.5 4.5 %collective-permute-done.37 = f32[2,64,8,128]{3,2,1,0:T(8,128)S(1)} collective-permute-done((f32[2,64,8,128]{3,2,1,0:T(8,128)S(1)}, f32[2,64,8,128]{3,2,1,0:T(8,128)S(1)}, u32[]{:S(2)}, u32[]{:S(2)}) %collective-permute-start.37) | collective-permute-done | bytes 524320 | tf_op jit(solution)/shard_map/ppermute | solution.py:476
  62.0 4.8 %collective-permute-start.15 = (f32[2,64,8,128]{3,2,1,0:T(8,128)S(1)}, f32[2,64,8,128]{3,2,1,0:T(8,128)S(1)}, u32[]{:S(2)}, u32[]{:S(2)}) collective-permute-start(f32[2,64,8,128]{3,2,1,0:T(8,128)S(1)} %get-tuple-element.177), channel_id=1, source_target_pairs={{0,2},{1,7},{2,0},{3,5},{4,6},{5,3},{6,4},{7,1},{8,10},{9,15},{10,... | collective-permute-start | bytes 1572872 | tf_op jit(solution)/shard_map/ppermute | solution.py:476
  75.6 5.5 %collective-permute-done.45 = f32[2,64,8,128]{3,2,1,0:T(8,128)S(1)} collective-permute-done((f32[2,64,8,128]{3,2,1,0:T(8,128)S(1)}, f32[2,64,8,128]{3,2,1,0:T(8,128)S(1)}, u32[]{:S(2)}, u32[]{:S(2)}) %collective-permute-start.45) | collective-permute-done | bytes 524320 | tf_op jit(solution)/shard_map/ppermute | solution.py:476
  83.5 3.0 %collective-permute-done.9 = f32[2,64,8,128]{3,2,1,0:T(8,128)S(1)} collective-permute-done((f32[2,64,8,128]{3,2,1,0:T(8,128)S(1)}, f32[2,64,8,128]{3,2,1,0:T(8,128)S(1)}, u32[]{:S(2)}, u32[]{:S(2)}) %collective-permute-start.9) | collective-permute-done | bytes 524320 | tf_op jit(solution)/shard_map/ppermute | solution.py:476
  86.5 3.3 %collective-permute-start.46 = (f32[2,64,8,128]{3,2,1,0:T(8,128)S(1)}, f32[2,64,8,128]{3,2,1,0:T(8,128)S(1)}, u32[]{:S(2)}, u32[]{:S(2)}) collective-permute-start(f32[2,64,8,128]{3,2,1,0:T(8,128)S(1)} %get-tuple-element.244), channel_id=1, source_target_pairs={{0,2},{1,7},{2,0},{3,5},{4,6},{5,3},{6,4},{7,1},{8,10},{9,15},{10,... | collective-permute-start | bytes 1572872 | tf_op jit(solution)/shard_map/ppermute | solution.py:476
  90.0 2.9 %collective-permute-done.22 = f32[2,64,8,128]{3,2,1,0:T(8,128)S(1)} collective-permute-done((f32[2,64,8,128]{3,2,1,0:T(8,128)S(1)}, f32[2,64,8,128]{3,2,1,0:T(8,128)S(1)}, u32[]{:S(2)}, u32[]{:S(2)}) %collective-permute-start.22) | collective-permute-done | bytes 524320 | tf_op jit(solution)/shard_map/ppermute | solution.py:476
  93.7 3.3 %collective-permute-done.53 = f32[2,64,8,128]{3,2,1,0:T(8,128)S(1)} collective-permute-done((f32[2,64,8,128]{3,2,1,0:T(8,128)S(1)}, f32[2,64,8,128]{3,2,1,0:T(8,128)S(1)}, u32[]{:S(2)}, u32[]{:S(2)}) %collective-permute-start.53) | collective-permute-done | bytes 524320 | tf_op jit(solution)/shard_map/ppermute | solution.py:476
  97.1 5.1 %collective-permute-done.46 = f32[2,64,8,128]{3,2,1,0:T(8,128)S(1)} collective-permute-done((f32[2,64,8,128]{3,2,1,0:T(8,128)S(1)}, f32[2,64,8,128]{3,2,1,0:T(8,128)S(1)}, u32[]{:S(2)}, u32[]{:S(2)}) %collective-permute-start.46) | collective-permute-done | bytes 524320 | tf_op jit(solution)/shard_map/ppermute | solution.py:476
  102.2 2.7 %collective-permute-start.23 = (f32[2,64,8,128]{3,2,1,0:T(8,128)S(1)}, f32[2,64,8,128]{3,2,1,0:T(8,128)S(1)}, u32[]{:S(2)}, u32[]{:S(2)}) collective-permute-start(f32[2,64,8,128]{3,2,1,0:T(8,128)S(1)} %get-tuple-element.193), channel_id=1, source_target_pairs={{0,2},{1,7},{2,0},{3,5},{4,6},{5,3},{6,4},{7,1},{8,10},{9,15},{10,... | collective-permute-start | bytes 1572872 | tf_op jit(solution)/shard_map/ppermute | solution.py:476
  105.4 8.1 %collective-permute-done.10 = f32[2,64,8,128]{3,2,1,0:T(8,128)S(1)} collective-permute-done((f32[2,64,8,128]{3,2,1,0:T(8,128)S(1)}, f32[2,64,8,128]{3,2,1,0:T(8,128)S(1)}, u32[]{:S(2)}, u32[]{:S(2)}) %collective-permute-start.10) | collective-permute-done | bytes 524320 | tf_op jit(solution)/shard_map/ppermute | solution.py:476
  116.4 4.8 %collective-permute-done.23 = f32[2,64,8,128]{3,2,1,0:T(8,128)S(1)} collective-permute-done((f32[2,64,8,128]{3,2,1,0:T(8,128)S(1)}, f32[2,64,8,128]{3,2,1,0:T(8,128)S(1)}, u32[]{:S(2)}, u32[]{:S(2)}) %collective-permute-start.23) | collective-permute-done | bytes 524320 | tf_op jit(solution)/shard_map/ppermute | solution.py:476
  124.1 3.9 %collective-permute-done.47 = f32[2,64,8,128]{3,2,1,0:T(8,128)S(1)} collective-permute-done((f32[2,64,8,128]{3,2,1,0:T(8,128)S(1)}, f32[2,64,8,128]{3,2,1,0:T(8,128)S(1)}, u32[]{:S(2)}, u32[]{:S(2)}) %collective-permute-start.47) | collective-permute-done | bytes 524320 | tf_op jit(solution)/shard_map/ppermute | solution.py:476
  128.1 11.2 %collective-permute-done.40 = f32[2,64,8,128]{3,2,1,0:T(8,128)S(1)} collective-permute-done((f32[2,64,8,128]{3,2,1,0:T(8,128)S(1)}, f32[2,64,8,128]{3,2,1,0:T(8,128)S(1)}, u32[]{:S(2)}, u32[]{:S(2)}) %collective-permute-start.40) | collective-permute-done | bytes 524320 | tf_op jit(solution)/shard_map/ppermute | solution.py:476
  139.4 12.6 %collective-permute-start.55 = (f32[2,64,8,128]{3,2,1,0:T(8,128)S(1)}, f32[2,64,8,128]{3,2,1,0:T(8,128)S(1)}, u32[]{:S(2)}, u32[]{:S(2)}) collective-permute-start(f32[2,64,8,128]{3,2,1,0:T(8,128)S(1)} %get-tuple-element.262), channel_id=1, source_target_pairs={{0,1},{1,0},{2,3},{3,2},{4,5},{5,4},{6,7},{7,6},{8,9},{9,8},{10,11... | collective-permute-start | bytes 1572872 | tf_op jit(solution)/shard_map/ppermute | solution.py:476
  162.6 3.4 %collective-permute-done.25 = f32[2,64,8,128]{3,2,1,0:T(8,128)S(1)} collective-permute-done((f32[2,64,8,128]{3,2,1,0:T(8,128)S(1)}, f32[2,64,8,128]{3,2,1,0:T(8,128)S(1)}, u32[]{:S(2)}, u32[]{:S(2)}) %collective-permute-start.25) | collective-permute-done | bytes 524320 | tf_op jit(solution)/shard_map/ppermute | solution.py:476
  168.2 5.1 %collective-permute-done.6 = f32[2,64,8,128]{3,2,1,0:T(8,128)S(1)} collective-permute-done((f32[2,64,8,128]{3,2,1,0:T(8,128)S(1)}, f32[2,64,8,128]{3,2,1,0:T(8,128)S(1)}, u32[]{:S(2)}, u32[]{:S(2)}) %collective-permute-start.6) | collective-permute-done | bytes 524320 | tf_op jit(solution)/shard_map/ppermute | solution.py:476
  174.9 2.8 %collective-permute-start.13 = (f32[2,64,8,128]{3,2,1,0:T(8,128)S(1)}, f32[2,64,8,128]{3,2,1,0:T(8,128)S(1)}, u32[]{:S(2)}, u32[]{:S(2)}) collective-permute-start(f32[2,64,8,128]{3,2,1,0:T(8,128)S(1)} %get-tuple-element.172), channel_id=1, source_target_pairs={{0,32},{1,97},{2,34},{3,99},{4,36},{5,101},{6,38},{7,103},{8,40},{... | collective-permute-start | bytes 1572872 | tf_op jit(solution)/shard_map/ppermute | solution.py:476
  (178 shorter events, 78.4 us)
Async XLA Ops:
  30.1 21.9 %collective-permute-start.1 = (f32[2,2,64,8,128]{4,3,2,1,0:T(8,128)S(1)}, f32[2,2,64,8,128]{4,3,2,1,0:T(8,128)S(1)}, u32[]{:S(2)}, u32[]{:S(2)}) collective-permute-start(f32[2,2,64,8,128]{4,3,2,1,0:T(8,128)S(1)} %get-tuple-element.147), channel_id=1, source_target_pairs={{0,1},{1,0},{2,3},{3,2},{4,5},{5,4},{6,7},{7,6},{8,9},{9,8},{10,11... | collective-permute-start | bytes 3145736 | tf_op jit(solution)/shard_map/ppermute | solution.py:476
  31.9 21.1 %collective-permute-start.14 = (f32[2,2,64,8,128]{4,3,2,1,0:T(8,128)S(1)}, f32[2,2,64,8,128]{4,3,2,1,0:T(8,128)S(1)}, u32[]{:S(2)}, u32[]{:S(2)}) collective-permute-start(f32[2,2,64,8,128]{4,3,2,1,0:T(8,128)S(1)} %get-tuple-element.175), channel_id=1, source_target_pairs={{0,1},{1,0},{2,3},{3,2},{4,5},{5,4},{6,7},{7,6},{8,9},{9,8},{10,11... | collective-permute-start | bytes 3145736 | tf_op jit(solution)/shard_map/ppermute | solution.py:476
  52.0 15.2 %collective-permute-start.30 = (f32[2,64,8,128]{3,2,1,0:T(8,128)S(1)}, f32[2,64,8,128]{3,2,1,0:T(8,128)S(1)}, u32[]{:S(2)}, u32[]{:S(2)}) collective-permute-start(f32[2,64,8,128]{3,2,1,0:T(8,128)S(1)} %get-tuple-element.209), channel_id=1, source_target_pairs={{0,32},{1,97},{2,34},{3,99},{4,36},{5,101},{6,38},{7,103},{8,40},{... | collective-permute-start | bytes 1572872 | tf_op jit(solution)/shard_map/ppermute | solution.py:476
  55.0 14.9 %collective-permute-start.21 = (f32[2,64,8,128]{3,2,1,0:T(8,128)S(1)}, f32[2,64,8,128]{3,2,1,0:T(8,128)S(1)}, u32[]{:S(2)}, u32[]{:S(2)}) collective-permute-start(f32[2,64,8,128]{3,2,1,0:T(8,128)S(1)} %get-tuple-element.189), channel_id=1, source_target_pairs={{0,96},{1,33},{2,98},{3,35},{4,100},{5,37},{6,102},{7,39},{8,104},... | collective-permute-start | bytes 1572872 | tf_op jit(solution)/shard_map/ppermute | solution.py:476
  82.3 14.7 %collective-permute-start.53 = (f32[2,64,8,128]{3,2,1,0:T(8,128)S(1)}, f32[2,64,8,128]{3,2,1,0:T(8,128)S(1)}, u32[]{:S(2)}, u32[]{:S(2)}) collective-permute-start(f32[2,64,8,128]{3,2,1,0:T(8,128)S(1)} %get-tuple-element.258), channel_id=1, source_target_pairs={{0,8},{1,25},{2,10},{3,27},{4,12},{5,29},{6,14},{7,31},{8,0},{9,17... | collective-permute-start | bytes 1572872 | tf_op jit(solution)/shard_map/ppermute | solution.py:476
  86.5 15.7 %collective-permute-start.46 = (f32[2,64,8,128]{3,2,1,0:T(8,128)S(1)}, f32[2,64,8,128]{3,2,1,0:T(8,128)S(1)}, u32[]{:S(2)}, u32[]{:S(2)}) collective-permute-start(f32[2,64,8,128]{3,2,1,0:T(8,128)S(1)} %get-tuple-element.244), channel_id=1, source_target_pairs={{0,2},{1,7},{2,0},{3,5},{4,6},{5,3},{6,4},{7,1},{8,10},{9,15},{10,... | collective-permute-start | bytes 1572872 | tf_op jit(solution)/shard_map/ppermute | solution.py:476
  89.8 15.2 %collective-permute-start.39 = (f32[2,64,8,128]{3,2,1,0:T(8,128)S(1)}, f32[2,64,8,128]{3,2,1,0:T(8,128)S(1)}, u32[]{:S(2)}, u32[]{:S(2)}) collective-permute-start(f32[2,64,8,128]{3,2,1,0:T(8,128)S(1)} %get-tuple-element.227), channel_id=1, source_target_pairs={{0,6},{1,3},{2,4},{3,1},{4,2},{5,7},{6,0},{7,5},{8,14},{9,11},{10,... | collective-permute-start | bytes 1572872 | tf_op jit(solution)/shard_map/ppermute | solution.py:476
  93.0 20.5 %collective-permute-start.10 = (f32[2,64,8,128]{3,2,1,0:T(8,128)S(1)}, f32[2,64,8,128]{3,2,1,0:T(8,128)S(1)}, u32[]{:S(2)}, u32[]{:S(2)}) collective-permute-start(f32[2,64,8,128]{3,2,1,0:T(8,128)S(1)} %get-tuple-element.166), channel_id=1, source_target_pairs={{0,2},{1,7},{2,0},{3,5},{4,6},{5,3},{6,4},{7,1},{8,10},{9,15},{10,... | collective-permute-start | bytes 1572872 | tf_op jit(solution)/shard_map/ppermute | solution.py:476
  97.0 17.4 %collective-permute-start.4 = (f32[2,64,8,128]{3,2,1,0:T(8,128)S(1)}, f32[2,64,8,128]{3,2,1,0:T(8,128)S(1)}, u32[]{:S(2)}, u32[]{:S(2)}) collective-permute-start(f32[2,64,8,128]{3,2,1,0:T(8,128)S(1)} %get-tuple-element.153), channel_id=1, source_target_pairs={{0,96},{1,33},{2,98},{3,35},{4,100},{5,37},{6,102},{7,39},{8,104},... | collective-permute-start | bytes 1572872 | tf_op jit(solution)/shard_map/ppermute | solution.py:476
  102.2 19.0 %collective-permute-start.23 = (f32[2,64,8,128]{3,2,1,0:T(8,128)S(1)}, f32[2,64,8,128]{3,2,1,0:T(8,128)S(1)}, u32[]{:S(2)}, u32[]{:S(2)}) collective-permute-start(f32[2,64,8,128]{3,2,1,0:T(8,128)S(1)} %get-tuple-element.193), channel_id=1, source_target_pairs={{0,2},{1,7},{2,0},{3,5},{4,6},{5,3},{6,4},{7,1},{8,10},{9,15},{10,... | collective-permute-start | bytes 1572872 | tf_op jit(solution)/shard_map/ppermute | solution.py:476
  105.0 16.3 %collective-permute-start.17 = (f32[2,64,8,128]{3,2,1,0:T(8,128)S(1)}, f32[2,64,8,128]{3,2,1,0:T(8,128)S(1)}, u32[]{:S(2)}, u32[]{:S(2)}) collective-permute-start(f32[2,64,8,128]{3,2,1,0:T(8,128)S(1)} %get-tuple-element.181), channel_id=1, source_target_pairs={{0,96},{1,33},{2,98},{3,35},{4,100},{5,37},{6,102},{7,39},{8,104},... | collective-permute-start | bytes 1572872 | tf_op jit(solution)/shard_map/ppermute | solution.py:476
  105.2 18.8 %collective-permute-start.54 = (f32[2,64,8,128]{3,2,1,0:T(8,128)S(1)}, f32[2,64,8,128]{3,2,1,0:T(8,128)S(1)}, u32[]{:S(2)}, u32[]{:S(2)}) collective-permute-start(f32[2,64,8,128]{3,2,1,0:T(8,128)S(1)} %get-tuple-element.260), channel_id=1, source_target_pairs={{0,6},{1,3},{2,4},{3,1},{4,2},{5,7},{6,0},{7,5},{8,14},{9,11},{10,... | collective-permute-start | bytes 1572872 | tf_op jit(solution)/shard_map/ppermute | solution.py:476
  114.4 24.8 %collective-permute-start.40 = (f32[2,64,8,128]{3,2,1,0:T(8,128)S(1)}, f32[2,64,8,128]{3,2,1,0:T(8,128)S(1)}, u32[]{:S(2)}, u32[]{:S(2)}) collective-permute-start(f32[2,64,8,128]{3,2,1,0:T(8,128)S(1)} %get-tuple-element.229), channel_id=1, source_target_pairs={{0,32},{1,97},{2,34},{3,99},{4,36},{5,101},{6,38},{7,103},{8,40},{... | collective-permute-start | bytes 1572872 | tf_op jit(solution)/shard_map/ppermute | solution.py:476
  121.2 18.2 %collective-permute-start.11 = (f32[2,64,8,128]{3,2,1,0:T(8,128)S(1)}, f32[2,64,8,128]{3,2,1,0:T(8,128)S(1)}, u32[]{:S(2)}, u32[]{:S(2)}) collective-permute-start(f32[2,64,8,128]{3,2,1,0:T(8,128)S(1)} %get-tuple-element.168), channel_id=1, source_target_pairs={{0,96},{1,33},{2,98},{3,35},{4,100},{5,37},{6,102},{7,39},{8,104},... | collective-permute-start | bytes 1572872 | tf_op jit(solution)/shard_map/ppermute | solution.py:476
  121.3 30.8 %collective-permute-start.24 = (f32[2,64,8,128]{3,2,1,0:T(8,128)S(1)}, f32[2,64,8,128]{3,2,1,0:T(8,128)S(1)}, u32[]{:S(2)}, u32[]{:S(2)}) collective-permute-start(f32[2,64,8,128]{3,2,1,0:T(8,128)S(1)} %get-tuple-element.195), channel_id=1, source_target_pairs={{0,32},{1,97},{2,34},{3,99},{4,36},{5,101},{6,38},{7,103},{8,40},{... | collective-permute-start | bytes 1572872 | tf_op jit(solution)/shard_map/ppermute | solution.py:476
  124.0 30.0 %collective-permute-start.18 = (f32[2,64,8,128]{3,2,1,0:T(8,128)S(1)}, f32[2,64,8,128]{3,2,1,0:T(8,128)S(1)}, u32[]{:S(2)}, u32[]{:S(2)}) collective-permute-start(f32[2,64,8,128]{3,2,1,0:T(8,128)S(1)} %get-tuple-element.183), channel_id=1, source_target_pairs={{0,24},{1,9},{2,26},{3,11},{4,28},{5,13},{6,30},{7,15},{8,16},{9,1... | collective-permute-start | bytes 1572872 | tf_op jit(solution)/shard_map/ppermute | solution.py:476
  128.1 28.6 %collective-permute-start.5 = (f32[2,64,8,128]{3,2,1,0:T(8,128)S(1)}, f32[2,64,8,128]{3,2,1,0:T(8,128)S(1)}, u32[]{:S(2)}, u32[]{:S(2)}) collective-permute-start(f32[2,64,8,128]{3,2,1,0:T(8,128)S(1)} %get-tuple-element.155), channel_id=1, source_target_pairs={{0,32},{1,97},{2,34},{3,99},{4,36},{5,101},{6,38},{7,103},{8,40},{... | collective-permute-start | bytes 1572872 | tf_op jit(solution)/shard_map/ppermute | solution.py:476
  139.3 17.7 %collective-permute-start.33 = (f32[2,64,8,128]{3,2,1,0:T(8,128)S(1)}, f32[2,64,8,128]{3,2,1,0:T(8,128)S(1)}, u32[]{:S(2)}, u32[]{:S(2)}) collective-permute-start(f32[2,64,8,128]{3,2,1,0:T(8,128)S(1)} %get-tuple-element.215), channel_id=1, source_target_pairs={{0,6},{1,3},{2,4},{3,1},{4,2},{5,7},{6,0},{7,5},{8,14},{9,11},{10,... | collective-permute-start | bytes 1572872 | tf_op jit(solution)/shard_map/ppermute | solution.py:476
  139.4 20.2 %collective-permute-start.55 = (f32[2,64,8,128]{3,2,1,0:T(8,128)S(1)}, f32[2,64,8,128]{3,2,1,0:T(8,128)S(1)}, u32[]{:S(2)}, u32[]{:S(2)}) collective-permute-start(f32[2,64,8,128]{3,2,1,0:T(8,128)S(1)} %get-tuple-element.262), channel_id=1, source_target_pairs={{0,1},{1,0},{2,3},{3,2},{4,5},{5,4},{6,7},{7,6},{8,9},{9,8},{10,11... | collective-permute-start | bytes 1572872 | tf_op jit(solution)/shard_map/ppermute | solution.py:476
  157.0 16.3 %collective-permute-start.6 = (f32[2,64,8,128]{3,2,1,0:T(8,128)S(1)}, f32[2,64,8,128]{3,2,1,0:T(8,128)S(1)}, u32[]{:S(2)}, u32[]{:S(2)}) collective-permute-start(f32[2,64,8,128]{3,2,1,0:T(8,128)S(1)} %get-tuple-element.157), channel_id=1, source_target_pairs={{0,8},{1,25},{2,10},{3,27},{4,12},{5,29},{6,14},{7,31},{8,0},{9,17... | collective-permute-start | bytes 1572872 | tf_op jit(solution)/shard_map/ppermute | solution.py:476
  159.6 15.3 %collective-permute-start.48 = (f32[2,64,8,128]{3,2,1,0:T(8,128)S(1)}, f32[2,64,8,128]{3,2,1,0:T(8,128)S(1)}, u32[]{:S(2)}, u32[]{:S(2)}) collective-permute-start(f32[2,64,8,128]{3,2,1,0:T(8,128)S(1)} %get-tuple-element.248), channel_id=1, source_target_pairs={{0,1},{1,0},{2,3},{3,2},{4,5},{5,4},{6,7},{7,6},{8,9},{9,8},{10,11... | collective-permute-start | bytes 1572872 | tf_op jit(solution)/shard_map/ppermute | solution.py:476
  160.8 18.1 %collective-permute-start.41 = (f32[2,64,8,128]{3,2,1,0:T(8,128)S(1)}, f32[2,64,8,128]{3,2,1,0:T(8,128)S(1)}, u32[]{:S(2)}, u32[]{:S(2)}) collective-permute-start(f32[2,64,8,128]{3,2,1,0:T(8,128)S(1)} %get-tuple-element.231), channel_id=1, source_target_pairs={{0,1},{1,0},{2,3},{3,2},{4,5},{5,4},{6,7},{7,6},{8,9},{9,8},{10,11... | collective-permute-start | bytes 1572872 | tf_op jit(solution)/shard_map/ppermute | solution.py:476
  166.0 17.2 %collective-permute-start.34 = (f32[2,64,8,128]{3,2,1,0:T(8,128)S(1)}, f32[2,64,8,128]{3,2,1,0:T(8,128)S(1)}, u32[]{:S(2)}, u32[]{:S(2)}) collective-permute-start(f32[2,64,8,128]{3,2,1,0:T(8,128)S(1)} %get-tuple-element.217), channel_id=1, source_target_pairs={{0,1},{1,0},{2,3},{3,2},{4,5},{5,4},{6,7},{7,6},{8,9},{9,8},{10,11... | collective-permute-start | bytes 1572872 | tf_op jit(solution)/shard_map/ppermute | solution.py:476
  167.7 16.8 %collective-permute-start.26 = (f32[2,64,8,128]{3,2,1,0:T(8,128)S(1)}, f32[2,64,8,128]{3,2,1,0:T(8,128)S(1)}, u32[]{:S(2)}, u32[]{:S(2)}) collective-permute-start(f32[2,64,8,128]{3,2,1,0:T(8,128)S(1)} %get-tuple-element.199), channel_id=1, source_target_pairs={{0,8},{1,25},{2,10},{3,27},{4,12},{5,29},{6,14},{7,31},{8,0},{9,17... | collective-permute-start | bytes 1572872 | tf_op jit(solution)/shard_map/ppermute | solution.py:476
  (35 other events, 389.6 us)

commit v3 on v2

--- a/solution.py
+++ b/solution.py
@@ -56,24 +56,28 @@
     return pairs
 
 
-def peer(me, frame, core, traveller, steps):
-    masks = [sum(bit << edge for bit, edge in zip(steps, edges_of(frame, c))) for c in range(2)]
-    return recode(recode(me // 2) ^ jnp.where(traveller == 0, *masks)) * 2 + core
-
-
-def targets(me, frame):
-    slot = jnp.arange(2 * SLOTS, dtype=jnp.int32)
-    core = me % 2 ^ slot >> STEPS
-    steps = [slot >> (STEPS - 1 - k) & 1 for k in range(STEPS)]
-    return peer(me, frame, core, me % 2 if frame in LATE else core, steps)
-
-
-def sources(me, frame):
-    slot = jnp.arange(2 * SLOTS, dtype=jnp.int32)
-    if frame in LATE:
-        core = me % 2 ^ slot >> STEPS
-        return peer(me, frame, core, core, [slot >> k & 1 for k in range(STEPS)])
-    return peer(me, frame, me % 2 ^ slot & 1, me % 2, [slot >> (k + 1) & 1 for k in range(STEPS)])
+def routes(forward):
+    slot = np.arange(2 * SLOTS)
+    masks, other = np.zeros((2, FRAMES, 2 * SLOTS), np.int32), np.zeros((FRAMES, 2 * SLOTS), np.int32)
+    for frame in range(FRAMES):
+        late = frame in LATE
+        other[frame] = slot >> STEPS if forward or late else slot & 1
+        for core in range(2):
+            if forward:
+                traveller = core + 0 * slot if late else core ^ other[frame]
+            else:
+                traveller = core ^ other[frame] if late else core + 0 * slot
+            for k in range(STEPS):
+                place = STEPS - 1 - k if forward else k if late else k + 1
+                edge = np.where(traveller == 0, edges_of(frame, 0)[k], edges_of(frame, 1)[k])
+                masks[core, frame] |= (slot >> place & 1) << edge
+    return (masks, other) if forward else (masks.transpose(0, 2, 1), other.T)
+
+
+def devices(me, forward):
+    masks, other = routes(forward)
+    mask = jnp.where(me % 2 == 0, jnp.asarray(masks[0]), jnp.asarray(masks[1]))
+    return recode(recode(me // 2) ^ mask) * 2 + (me % 2 ^ jnp.asarray(other))
 
 
 def hamming(index):
@@ -495,8 +499,7 @@
     row = jnp.broadcast_to(row[:, None, None], (rows, SUB, LANES)).reshape(rows * SUB, LANES)
     col = jnp.asarray(column_window())
     tw = jnp.asarray(twiddles())
-    target = jnp.stack([targets(me, f) for f in range(frames)])
-    source = jnp.stack([sources(me, f) for f in range(frames)], axis=1)
+    target, source = devices(me, True), devices(me, False)
     z, forward, backward = short(real, imag, col, tw, target, source)
     edge = [edges(halo, col, tw) for halo in halos]
     halves = []

time: 192 us -> 192 us (level)
  no operation moved by 1% of the time
where the time goes in v3:
time: 192 us
  waiting for transfers between devices  82.2 us (43%)
  starting transfers between devices  79.2 us (41%)
  Pallas kernels  28.2 us (15%)
    ppermute x56, waiting for transfers between devices, permute(): return lax.ppermute(value, 'pa', pairs)  82.2 us
    ppermute x56, starting transfers between devices, permute(): return lax.ppermute(value, 'pa', pairs)  79.2 us
    pallas_call x8, Pallas kernels, post(): pl.pallas_call(functools.partial(post_kernel, frame=frame), in_specs=[VME...  9.28 us
    pallas_call x4, Pallas kernels, pre(): pl.pallas_call(functools.partial(pre_kernel, first=first), grid=(count,),...  6.87 us
    pallas_call x1, Pallas kernels, short(): pl.pallas_call(short_kernel, in_specs=[ANY] * 2 + [VMEM] * 5, out_specs=[...  5.01 us
    pallas_call x52, Pallas kernels, gather(): pl.pallas_call(kernel, in_specs=[VMEM] * 2, out_specs=[VMEM] * 2, out_sha...  4.09 us
  transfers between devices with their start and end apart: 56, of which 28 were waited for; matrix products, arithmetic and copies ran while one was open for 0% of the time, Pallas kernels for 12%

profile of v3, /device:TPU:1, one launch (start us, length us, event | category | flops | bytes accessed | tf_op | source)
XLA Modules:
  0.0 191.8 jit_solution(9885548340648087671)
XLA Ops:
  2.5 4.6 %collective-permute-start.27 = (f32[2,8,4096]{2,1,0:T(8,128)S(1)}, f32[2,8,4096]{2,1,0:T(8,128)S(1)}, u32[]{:S(2)}, u32[]{:S(2)}) collective-permute-start(f32[2,8,4096]{2,1,0:T(8,128)S(1)} %get-tuple-element.201), channel_id=1, source_target_pairs={{0,1},{1,2},{2,3},{3,4},{4,5},{5,6},{6,7},{7,8},{8,9},{9,10},{10,1... | collective-permute-start | bytes 786440 | tf_op jit(solution)/shard_map/ppermute | solution.py:480
  7.5 5.0 %short.1 = (f32[2,2,1024,128]{3,2,1,0:T(8,128)S(1)}, f32[2,2,1024,128]{3,2,1,0:T(8,128)S(1)}, f32[2,2,1024,128]{3,2,1,0:T(8,128)S(1)}, f32[2,2,1024,128]{3,2,1,0...) custom-call(f32[8,32,4096]{2,1,0:T(8,128)} %real_ref.3, ...), custom_call_target="tpu_custom_call" | custom-call | flops 1000000000 | bytes 2097152 | tf_op jit(solution)/shard_map/short/pallas_call | solution.py:379
  19.1 3.8 %collective-permute-start.42 = (f32[2,64,8,128]{3,2,1,0:T(8,128)S(1)}, f32[2,64,8,128]{3,2,1,0:T(8,128)S(1)}, u32[]{:S(2)}, u32[]{:S(2)}) collective-permute-start(f32[2,64,8,128]{3,2,1,0:T(8,128)S(1)} %get-tuple-element.236), channel_id=1, source_target_pairs={{0,8},{1,25},{2,10},{3,27},{4,12},{5,29},{6,14},{7,31},{8,0},{9,17... | collective-permute-start | bytes 1572872 | tf_op jit(solution)/shard_map/ppermute | solution.py:480
  24.8 3.1 %collective-permute-start.35 = (f32[2,64,8,128]{3,2,1,0:T(8,128)S(1)}, f32[2,64,8,128]{3,2,1,0:T(8,128)S(1)}, u32[]{:S(2)}, u32[]{:S(2)}) collective-permute-start(f32[2,64,8,128]{3,2,1,0:T(8,128)S(1)} %get-tuple-element.219), channel_id=1, source_target_pairs={{0,2},{1,7},{2,0},{3,5},{4,6},{5,3},{6,4},{7,1},{8,10},{9,15},{10,... | collective-permute-start | bytes 1572872 | tf_op jit(solution)/shard_map/ppermute | solution.py:480
  34.5 2.6 %collective-permute-start.43 = (f32[2,64,8,128]{3,2,1,0:T(8,128)S(1)}, f32[2,64,8,128]{3,2,1,0:T(8,128)S(1)}, u32[]{:S(2)}, u32[]{:S(2)}) collective-permute-start(f32[2,64,8,128]{3,2,1,0:T(8,128)S(1)} %get-tuple-element.238), channel_id=1, source_target_pairs={{0,96},{1,33},{2,98},{3,35},{4,100},{5,37},{6,102},{7,39},{8,104},... | collective-permute-start | bytes 1572872 | tf_op jit(solution)/shard_map/ppermute | solution.py:480
  40.4 2.7 %collective-permute-start.29 = (f32[2,64,8,128]{3,2,1,0:T(8,128)S(1)}, f32[2,64,8,128]{3,2,1,0:T(8,128)S(1)}, u32[]{:S(2)}, u32[]{:S(2)}) collective-permute-start(f32[2,64,8,128]{3,2,1,0:T(8,128)S(1)} %get-tuple-element.207), channel_id=1, source_target_pairs={{0,2},{1,7},{2,0},{3,5},{4,6},{5,3},{6,4},{7,1},{8,10},{9,15},{10,... | collective-permute-start | bytes 1572872 | tf_op jit(solution)/shard_map/ppermute | solution.py:480
  46.7 3.0 %collective-permute-done.29 = f32[2,64,8,128]{3,2,1,0:T(8,128)S(1)} collective-permute-done((f32[2,64,8,128]{3,2,1,0:T(8,128)S(1)}, f32[2,64,8,128]{3,2,1,0:T(8,128)S(1)}, u32[]{:S(2)}, u32[]{:S(2)}) %collective-permute-start.29) | collective-permute-done | bytes 524320 | tf_op jit(solution)/shard_map/ppermute | solution.py:480
  57.6 4.5 %collective-permute-done.37 = f32[2,64,8,128]{3,2,1,0:T(8,128)S(1)} collective-permute-done((f32[2,64,8,128]{3,2,1,0:T(8,128)S(1)}, f32[2,64,8,128]{3,2,1,0:T(8,128)S(1)}, u32[]{:S(2)}, u32[]{:S(2)}) %collective-permute-start.37) | collective-permute-done | bytes 524320 | tf_op jit(solution)/shard_map/ppermute | solution.py:480
  62.1 4.8 %collective-permute-start.15 = (f32[2,64,8,128]{3,2,1,0:T(8,128)S(1)}, f32[2,64,8,128]{3,2,1,0:T(8,128)S(1)}, u32[]{:S(2)}, u32[]{:S(2)}) collective-permute-start(f32[2,64,8,128]{3,2,1,0:T(8,128)S(1)} %get-tuple-element.177), channel_id=1, source_target_pairs={{0,2},{1,7},{2,0},{3,5},{4,6},{5,3},{6,4},{7,1},{8,10},{9,15},{10,... | collective-permute-start | bytes 1572872 | tf_op jit(solution)/shard_map/ppermute | solution.py:480
  75.7 5.5 %collective-permute-done.45 = f32[2,64,8,128]{3,2,1,0:T(8,128)S(1)} collective-permute-done((f32[2,64,8,128]{3,2,1,0:T(8,128)S(1)}, f32[2,64,8,128]{3,2,1,0:T(8,128)S(1)}, u32[]{:S(2)}, u32[]{:S(2)}) %collective-permute-start.45) | collective-permute-done | bytes 524320 | tf_op jit(solution)/shard_map/ppermute | solution.py:480
  83.6 3.0 %collective-permute-done.9 = f32[2,64,8,128]{3,2,1,0:T(8,128)S(1)} collective-permute-done((f32[2,64,8,128]{3,2,1,0:T(8,128)S(1)}, f32[2,64,8,128]{3,2,1,0:T(8,128)S(1)}, u32[]{:S(2)}, u32[]{:S(2)}) %collective-permute-start.9) | collective-permute-done | bytes 524320 | tf_op jit(solution)/shard_map/ppermute | solution.py:480
  86.6 3.3 %collective-permute-start.46 = (f32[2,64,8,128]{3,2,1,0:T(8,128)S(1)}, f32[2,64,8,128]{3,2,1,0:T(8,128)S(1)}, u32[]{:S(2)}, u32[]{:S(2)}) collective-permute-start(f32[2,64,8,128]{3,2,1,0:T(8,128)S(1)} %get-tuple-element.244), channel_id=1, source_target_pairs={{0,2},{1,7},{2,0},{3,5},{4,6},{5,3},{6,4},{7,1},{8,10},{9,15},{10,... | collective-permute-start | bytes 1572872 | tf_op jit(solution)/shard_map/ppermute | solution.py:480
  90.1 2.9 %collective-permute-done.22 = f32[2,64,8,128]{3,2,1,0:T(8,128)S(1)} collective-permute-done((f32[2,64,8,128]{3,2,1,0:T(8,128)S(1)}, f32[2,64,8,128]{3,2,1,0:T(8,128)S(1)}, u32[]{:S(2)}, u32[]{:S(2)}) %collective-permute-start.22) | collective-permute-done | bytes 524320 | tf_op jit(solution)/shard_map/ppermute | solution.py:480
  93.9 2.9 %collective-permute-done.53 = f32[2,64,8,128]{3,2,1,0:T(8,128)S(1)} collective-permute-done((f32[2,64,8,128]{3,2,1,0:T(8,128)S(1)}, f32[2,64,8,128]{3,2,1,0:T(8,128)S(1)}, u32[]{:S(2)}, u32[]{:S(2)}) %collective-permute-start.53) | collective-permute-done | bytes 524320 | tf_op jit(solution)/shard_map/ppermute | solution.py:480
  96.9 5.4 %collective-permute-done.46 = f32[2,64,8,128]{3,2,1,0:T(8,128)S(1)} collective-permute-done((f32[2,64,8,128]{3,2,1,0:T(8,128)S(1)}, f32[2,64,8,128]{3,2,1,0:T(8,128)S(1)}, u32[]{:S(2)}, u32[]{:S(2)}) %collective-permute-start.46) | collective-permute-done | bytes 524320 | tf_op jit(solution)/shard_map/ppermute | solution.py:480
  102.3 2.7 %collective-permute-start.23 = (f32[2,64,8,128]{3,2,1,0:T(8,128)S(1)}, f32[2,64,8,128]{3,2,1,0:T(8,128)S(1)}, u32[]{:S(2)}, u32[]{:S(2)}) collective-permute-start(f32[2,64,8,128]{3,2,1,0:T(8,128)S(1)} %get-tuple-element.193), channel_id=1, source_target_pairs={{0,2},{1,7},{2,0},{3,5},{4,6},{5,3},{6,4},{7,1},{8,10},{9,15},{10,... | collective-permute-start | bytes 1572872 | tf_op jit(solution)/shard_map/ppermute | solution.py:480
  105.5 8.1 %collective-permute-done.10 = f32[2,64,8,128]{3,2,1,0:T(8,128)S(1)} collective-permute-done((f32[2,64,8,128]{3,2,1,0:T(8,128)S(1)}, f32[2,64,8,128]{3,2,1,0:T(8,128)S(1)}, u32[]{:S(2)}, u32[]{:S(2)}) %collective-permute-start.10) | collective-permute-done | bytes 524320 | tf_op jit(solution)/shard_map/ppermute | solution.py:480
  116.5 5.3 %collective-permute-done.23 = f32[2,64,8,128]{3,2,1,0:T(8,128)S(1)} collective-permute-done((f32[2,64,8,128]{3,2,1,0:T(8,128)S(1)}, f32[2,64,8,128]{3,2,1,0:T(8,128)S(1)}, u32[]{:S(2)}, u32[]{:S(2)}) %collective-permute-start.23) | collective-permute-done | bytes 524320 | tf_op jit(solution)/shard_map/ppermute | solution.py:480
  124.2 3.9 %collective-permute-done.47 = f32[2,64,8,128]{3,2,1,0:T(8,128)S(1)} collective-permute-done((f32[2,64,8,128]{3,2,1,0:T(8,128)S(1)}, f32[2,64,8,128]{3,2,1,0:T(8,128)S(1)}, u32[]{:S(2)}, u32[]{:S(2)}) %collective-permute-start.47) | collective-permute-done | bytes 524320 | tf_op jit(solution)/shard_map/ppermute | solution.py:480
  128.2 11.2 %collective-permute-done.40 = f32[2,64,8,128]{3,2,1,0:T(8,128)S(1)} collective-permute-done((f32[2,64,8,128]{3,2,1,0:T(8,128)S(1)}, f32[2,64,8,128]{3,2,1,0:T(8,128)S(1)}, u32[]{:S(2)}, u32[]{:S(2)}) %collective-permute-start.40) | collective-permute-done | bytes 524320 | tf_op jit(solution)/shard_map/ppermute | solution.py:480
  139.5 12.6 %collective-permute-start.55 = (f32[2,64,8,128]{3,2,1,0:T(8,128)S(1)}, f32[2,64,8,128]{3,2,1,0:T(8,128)S(1)}, u32[]{:S(2)}, u32[]{:S(2)}) collective-permute-start(f32[2,64,8,128]{3,2,1,0:T(8,128)S(1)} %get-tuple-element.262), channel_id=1, source_target_pairs={{0,1},{1,0},{2,3},{3,2},{4,5},{5,4},{6,7},{7,6},{8,9},{9,8},{10,11... | collective-permute-start | bytes 1572872 | tf_op jit(solution)/shard_map/ppermute | solution.py:480
  162.8 3.4 %collective-permute-done.25 = f32[2,64,8,128]{3,2,1,0:T(8,128)S(1)} collective-permute-done((f32[2,64,8,128]{3,2,1,0:T(8,128)S(1)}, f32[2,64,8,128]{3,2,1,0:T(8,128)S(1)}, u32[]{:S(2)}, u32[]{:S(2)}) %collective-permute-start.25) | collective-permute-done | bytes 524320 | tf_op jit(solution)/shard_map/ppermute | solution.py:480
  167.9 5.5 %collective-permute-done.6 = f32[2,64,8,128]{3,2,1,0:T(8,128)S(1)} collective-permute-done((f32[2,64,8,128]{3,2,1,0:T(8,128)S(1)}, f32[2,64,8,128]{3,2,1,0:T(8,128)S(1)}, u32[]{:S(2)}, u32[]{:S(2)}) %collective-permute-start.6) | collective-permute-done | bytes 524320 | tf_op jit(solution)/shard_map/ppermute | solution.py:480
  175.0 2.8 %collective-permute-start.13 = (f32[2,64,8,128]{3,2,1,0:T(8,128)S(1)}, f32[2,64,8,128]{3,2,1,0:T(8,128)S(1)}, u32[]{:S(2)}, u32[]{:S(2)}) collective-permute-start(f32[2,64,8,128]{3,2,1,0:T(8,128)S(1)} %get-tuple-element.172), channel_id=1, source_target_pairs={{0,32},{1,97},{2,34},{3,99},{4,36},{5,101},{6,38},{7,103},{8,40},{... | collective-permute-start | bytes 1572872 | tf_op jit(solution)/shard_map/ppermute | solution.py:480
  (181 shorter events, 77.2 us)
Async XLA Ops:
  30.2 21.9 %collective-permute-start.1 = (f32[2,2,64,8,128]{4,3,2,1,0:T(8,128)S(1)}, f32[2,2,64,8,128]{4,3,2,1,0:T(8,128)S(1)}, u32[]{:S(2)}, u32[]{:S(2)}) collective-permute-start(f32[2,2,64,8,128]{4,3,2,1,0:T(8,128)S(1)} %get-tuple-element.147), channel_id=1, source_target_pairs={{0,1},{1,0},{2,3},{3,2},{4,5},{5,4},{6,7},{7,6},{8,9},{9,8},{10,11... | collective-permute-start | bytes 3145736 | tf_op jit(solution)/shard_map/ppermute | solution.py:480
  32.0 21.1 %collective-permute-start.14 = (f32[2,2,64,8,128]{4,3,2,1,0:T(8,128)S(1)}, f32[2,2,64,8,128]{4,3,2,1,0:T(8,128)S(1)}, u32[]{:S(2)}, u32[]{:S(2)}) collective-permute-start(f32[2,2,64,8,128]{4,3,2,1,0:T(8,128)S(1)} %get-tuple-element.175), channel_id=1, source_target_pairs={{0,1},{1,0},{2,3},{3,2},{4,5},{5,4},{6,7},{7,6},{8,9},{9,8},{10,11... | collective-permute-start | bytes 3145736 | tf_op jit(solution)/shard_map/ppermute | solution.py:480
  52.1 15.2 %collective-permute-start.30 = (f32[2,64,8,128]{3,2,1,0:T(8,128)S(1)}, f32[2,64,8,128]{3,2,1,0:T(8,128)S(1)}, u32[]{:S(2)}, u32[]{:S(2)}) collective-permute-start(f32[2,64,8,128]{3,2,1,0:T(8,128)S(1)} %get-tuple-element.209), channel_id=1, source_target_pairs={{0,32},{1,97},{2,34},{3,99},{4,36},{5,101},{6,38},{7,103},{8,40},{... | collective-permute-start | bytes 1572872 | tf_op jit(solution)/shard_map/ppermute | solution.py:480
  53.2 14.6 %collective-permute-start.8 = (f32[2,64,8,128]{3,2,1,0:T(8,128)S(1)}, f32[2,64,8,128]{3,2,1,0:T(8,128)S(1)}, u32[]{:S(2)}, u32[]{:S(2)}) collective-permute-start(f32[2,64,8,128]{3,2,1,0:T(8,128)S(1)} %get-tuple-element.162), channel_id=1, source_target_pairs={{0,8},{1,25},{2,10},{3,27},{4,12},{5,29},{6,14},{7,31},{8,0},{9,17... | collective-permute-start | bytes 1572872 | tf_op jit(solution)/shard_map/ppermute | solution.py:480
  55.1 14.9 %collective-permute-start.21 = (f32[2,64,8,128]{3,2,1,0:T(8,128)S(1)}, f32[2,64,8,128]{3,2,1,0:T(8,128)S(1)}, u32[]{:S(2)}, u32[]{:S(2)}) collective-permute-start(f32[2,64,8,128]{3,2,1,0:T(8,128)S(1)} %get-tuple-element.189), channel_id=1, source_target_pairs={{0,96},{1,33},{2,98},{3,35},{4,100},{5,37},{6,102},{7,39},{8,104},... | collective-permute-start | bytes 1572872 | tf_op jit(solution)/shard_map/ppermute | solution.py:480
  86.6 15.7 %collective-permute-start.46 = (f32[2,64,8,128]{3,2,1,0:T(8,128)S(1)}, f32[2,64,8,128]{3,2,1,0:T(8,128)S(1)}, u32[]{:S(2)}, u32[]{:S(2)}) collective-permute-start(f32[2,64,8,128]{3,2,1,0:T(8,128)S(1)} %get-tuple-element.244), channel_id=1, source_target_pairs={{0,2},{1,7},{2,0},{3,5},{4,6},{5,3},{6,4},{7,1},{8,10},{9,15},{10,... | collective-permute-start | bytes 1572872 | tf_op jit(solution)/shard_map/ppermute | solution.py:480
  89.9 15.2 %collective-permute-start.39 = (f32[2,64,8,128]{3,2,1,0:T(8,128)S(1)}, f32[2,64,8,128]{3,2,1,0:T(8,128)S(1)}, u32[]{:S(2)}, u32[]{:S(2)}) collective-permute-start(f32[2,64,8,128]{3,2,1,0:T(8,128)S(1)} %get-tuple-element.227), channel_id=1, source_target_pairs={{0,6},{1,3},{2,4},{3,1},{4,2},{5,7},{6,0},{7,5},{8,14},{9,11},{10,... | collective-permute-start | bytes 1572872 | tf_op jit(solution)/shard_map/ppermute | solution.py:480
  93.1 20.5 %collective-permute-start.10 = (f32[2,64,8,128]{3,2,1,0:T(8,128)S(1)}, f32[2,64,8,128]{3,2,1,0:T(8,128)S(1)}, u32[]{:S(2)}, u32[]{:S(2)}) collective-permute-start(f32[2,64,8,128]{3,2,1,0:T(8,128)S(1)} %get-tuple-element.166), channel_id=1, source_target_pairs={{0,2},{1,7},{2,0},{3,5},{4,6},{5,3},{6,4},{7,1},{8,10},{9,15},{10,... | collective-permute-start | bytes 1572872 | tf_op jit(solution)/shard_map/ppermute | solution.py:480
  96.8 17.8 %collective-permute-start.4 = (f32[2,64,8,128]{3,2,1,0:T(8,128)S(1)}, f32[2,64,8,128]{3,2,1,0:T(8,128)S(1)}, u32[]{:S(2)}, u32[]{:S(2)}) collective-permute-start(f32[2,64,8,128]{3,2,1,0:T(8,128)S(1)} %get-tuple-element.153), channel_id=1, source_target_pairs={{0,96},{1,33},{2,98},{3,35},{4,100},{5,37},{6,102},{7,39},{8,104},... | collective-permute-start | bytes 1572872 | tf_op jit(solution)/shard_map/ppermute | solution.py:480
  102.3 19.5 %collective-permute-start.23 = (f32[2,64,8,128]{3,2,1,0:T(8,128)S(1)}, f32[2,64,8,128]{3,2,1,0:T(8,128)S(1)}, u32[]{:S(2)}, u32[]{:S(2)}) collective-permute-start(f32[2,64,8,128]{3,2,1,0:T(8,128)S(1)} %get-tuple-element.193), channel_id=1, source_target_pairs={{0,2},{1,7},{2,0},{3,5},{4,6},{5,3},{6,4},{7,1},{8,10},{9,15},{10,... | collective-permute-start | bytes 1572872 | tf_op jit(solution)/shard_map/ppermute | solution.py:480
  105.1 16.8 %collective-permute-start.17 = (f32[2,64,8,128]{3,2,1,0:T(8,128)S(1)}, f32[2,64,8,128]{3,2,1,0:T(8,128)S(1)}, u32[]{:S(2)}, u32[]{:S(2)}) collective-permute-start(f32[2,64,8,128]{3,2,1,0:T(8,128)S(1)} %get-tuple-element.181), channel_id=1, source_target_pairs={{0,96},{1,33},{2,98},{3,35},{4,100},{5,37},{6,102},{7,39},{8,104},... | collective-permute-start | bytes 1572872 | tf_op jit(solution)/shard_map/ppermute | solution.py:480
  105.3 18.8 %collective-permute-start.54 = (f32[2,64,8,128]{3,2,1,0:T(8,128)S(1)}, f32[2,64,8,128]{3,2,1,0:T(8,128)S(1)}, u32[]{:S(2)}, u32[]{:S(2)}) collective-permute-start(f32[2,64,8,128]{3,2,1,0:T(8,128)S(1)} %get-tuple-element.260), channel_id=1, source_target_pairs={{0,6},{1,3},{2,4},{3,1},{4,2},{5,7},{6,0},{7,5},{8,14},{9,11},{10,... | collective-permute-start | bytes 1572872 | tf_op jit(solution)/shard_map/ppermute | solution.py:480
  114.6 24.8 %collective-permute-start.40 = (f32[2,64,8,128]{3,2,1,0:T(8,128)S(1)}, f32[2,64,8,128]{3,2,1,0:T(8,128)S(1)}, u32[]{:S(2)}, u32[]{:S(2)}) collective-permute-start(f32[2,64,8,128]{3,2,1,0:T(8,128)S(1)} %get-tuple-element.229), channel_id=1, source_target_pairs={{0,32},{1,97},{2,34},{3,99},{4,36},{5,101},{6,38},{7,103},{8,40},{... | collective-permute-start | bytes 1572872 | tf_op jit(solution)/shard_map/ppermute | solution.py:480
  121.8 17.7 %collective-permute-start.11 = (f32[2,64,8,128]{3,2,1,0:T(8,128)S(1)}, f32[2,64,8,128]{3,2,1,0:T(8,128)S(1)}, u32[]{:S(2)}, u32[]{:S(2)}) collective-permute-start(f32[2,64,8,128]{3,2,1,0:T(8,128)S(1)} %get-tuple-element.168), channel_id=1, source_target_pairs={{0,96},{1,33},{2,98},{3,35},{4,100},{5,37},{6,102},{7,39},{8,104},... | collective-permute-start | bytes 1572872 | tf_op jit(solution)/shard_map/ppermute | solution.py:480
  121.9 30.3 %collective-permute-start.24 = (f32[2,64,8,128]{3,2,1,0:T(8,128)S(1)}, f32[2,64,8,128]{3,2,1,0:T(8,128)S(1)}, u32[]{:S(2)}, u32[]{:S(2)}) collective-permute-start(f32[2,64,8,128]{3,2,1,0:T(8,128)S(1)} %get-tuple-element.195), channel_id=1, source_target_pairs={{0,32},{1,97},{2,34},{3,99},{4,36},{5,101},{6,38},{7,103},{8,40},{... | collective-permute-start | bytes 1572872 | tf_op jit(solution)/shard_map/ppermute | solution.py:480
  124.1 30.0 %collective-permute-start.18 = (f32[2,64,8,128]{3,2,1,0:T(8,128)S(1)}, f32[2,64,8,128]{3,2,1,0:T(8,128)S(1)}, u32[]{:S(2)}, u32[]{:S(2)}) collective-permute-start(f32[2,64,8,128]{3,2,1,0:T(8,128)S(1)} %get-tuple-element.183), channel_id=1, source_target_pairs={{0,24},{1,9},{2,26},{3,11},{4,28},{5,13},{6,30},{7,15},{8,16},{9,1... | collective-permute-start | bytes 1572872 | tf_op jit(solution)/shard_map/ppermute | solution.py:480
  128.2 28.6 %collective-permute-start.5 = (f32[2,64,8,128]{3,2,1,0:T(8,128)S(1)}, f32[2,64,8,128]{3,2,1,0:T(8,128)S(1)}, u32[]{:S(2)}, u32[]{:S(2)}) collective-permute-start(f32[2,64,8,128]{3,2,1,0:T(8,128)S(1)} %get-tuple-element.155), channel_id=1, source_target_pairs={{0,32},{1,97},{2,34},{3,99},{4,36},{5,101},{6,38},{7,103},{8,40},{... | collective-permute-start | bytes 1572872 | tf_op jit(solution)/shard_map/ppermute | solution.py:480
  139.4 17.8 %collective-permute-start.33 = (f32[2,64,8,128]{3,2,1,0:T(8,128)S(1)}, f32[2,64,8,128]{3,2,1,0:T(8,128)S(1)}, u32[]{:S(2)}, u32[]{:S(2)}) collective-permute-start(f32[2,64,8,128]{3,2,1,0:T(8,128)S(1)} %get-tuple-element.215), channel_id=1, source_target_pairs={{0,6},{1,3},{2,4},{3,1},{4,2},{5,7},{6,0},{7,5},{8,14},{9,11},{10,... | collective-permute-start | bytes 1572872 | tf_op jit(solution)/shard_map/ppermute | solution.py:480
  139.5 20.2 %collective-permute-start.55 = (f32[2,64,8,128]{3,2,1,0:T(8,128)S(1)}, f32[2,64,8,128]{3,2,1,0:T(8,128)S(1)}, u32[]{:S(2)}, u32[]{:S(2)}) collective-permute-start(f32[2,64,8,128]{3,2,1,0:T(8,128)S(1)} %get-tuple-element.262), channel_id=1, source_target_pairs={{0,1},{1,0},{2,3},{3,2},{4,5},{5,4},{6,7},{7,6},{8,9},{9,8},{10,11... | collective-permute-start | bytes 1572872 | tf_op jit(solution)/shard_map/ppermute | solution.py:480
  157.2 16.3 %collective-permute-start.6 = (f32[2,64,8,128]{3,2,1,0:T(8,128)S(1)}, f32[2,64,8,128]{3,2,1,0:T(8,128)S(1)}, u32[]{:S(2)}, u32[]{:S(2)}) collective-permute-start(f32[2,64,8,128]{3,2,1,0:T(8,128)S(1)} %get-tuple-element.157), channel_id=1, source_target_pairs={{0,8},{1,25},{2,10},{3,27},{4,12},{5,29},{6,14},{7,31},{8,0},{9,17... | collective-permute-start | bytes 1572872 | tf_op jit(solution)/shard_map/ppermute | solution.py:480
  159.7 15.3 %collective-permute-start.48 = (f32[2,64,8,128]{3,2,1,0:T(8,128)S(1)}, f32[2,64,8,128]{3,2,1,0:T(8,128)S(1)}, u32[]{:S(2)}, u32[]{:S(2)}) collective-permute-start(f32[2,64,8,128]{3,2,1,0:T(8,128)S(1)} %get-tuple-element.248), channel_id=1, source_target_pairs={{0,1},{1,0},{2,3},{3,2},{4,5},{5,4},{6,7},{7,6},{8,9},{9,8},{10,11... | collective-permute-start | bytes 1572872 | tf_op jit(solution)/shard_map/ppermute | solution.py:480
  160.9 18.2 %collective-permute-start.41 = (f32[2,64,8,128]{3,2,1,0:T(8,128)S(1)}, f32[2,64,8,128]{3,2,1,0:T(8,128)S(1)}, u32[]{:S(2)}, u32[]{:S(2)}) collective-permute-start(f32[2,64,8,128]{3,2,1,0:T(8,128)S(1)} %get-tuple-element.231), channel_id=1, source_target_pairs={{0,1},{1,0},{2,3},{3,2},{4,5},{5,4},{6,7},{7,6},{8,9},{9,8},{10,11... | collective-permute-start | bytes 1572872 | tf_op jit(solution)/shard_map/ppermute | solution.py:480
  166.2 17.2 %collective-permute-start.34 = (f32[2,64,8,128]{3,2,1,0:T(8,128)S(1)}, f32[2,64,8,128]{3,2,1,0:T(8,128)S(1)}, u32[]{:S(2)}, u32[]{:S(2)}) collective-permute-start(f32[2,64,8,128]{3,2,1,0:T(8,128)S(1)} %get-tuple-element.217), channel_id=1, source_target_pairs={{0,1},{1,0},{2,3},{3,2},{4,5},{5,4},{6,7},{7,6},{8,9},{9,8},{10,11... | collective-permute-start | bytes 1572872 | tf_op jit(solution)/shard_map/ppermute | solution.py:480
  167.8 16.8 %collective-permute-start.26 = (f32[2,64,8,128]{3,2,1,0:T(8,128)S(1)}, f32[2,64,8,128]{3,2,1,0:T(8,128)S(1)}, u32[]{:S(2)}, u32[]{:S(2)}) collective-permute-start(f32[2,64,8,128]{3,2,1,0:T(8,128)S(1)} %get-tuple-element.199), channel_id=1, source_target_pairs={{0,8},{1,25},{2,10},{3,27},{4,12},{5,29},{6,14},{7,31},{8,0},{9,17... | collective-permute-start | bytes 1572872 | tf_op jit(solution)/shard_map/ppermute | solution.py:480
  (41 other events, 429.7 us)
